TPU v7x, 128 devices: a whole 4x4x4 slice. The times are simulated.
128 devices in a mesh: grp: 4 (over z), dev: 32 (over x, y, core).
Axes of the slice: x: 4, y: 4, z: 4, core: 2. Of those that a mesh axis runs over, the one named last changes fastest.
Arguments:
- matrix_tiles: bfloat16 [10240, 128, 1024], P(('grp', 'dev')), may hold values from -0.125 to 0.125
- tile_column: int32 [10240], P(('grp', 'dev')), may hold values from 0 to 255
- block_counts: int32 [4096], P(('grp', 'dev')), may hold values from 1 to 4, as said below
- destination: int32 [4096], P(('grp', 'dev')), may hold values from 0 to 31, as said below
- row_bounds: bfloat16 [524288], P(('grp', 'dev')), may hold values from -6 to 6
- dual_start: bfloat16 [524288], P(('grp', 'dev')), may hold values from 0 to 1
- primal_start: float32 [262144], replicated, may hold values from 0 to 0.5
- cost_vector: float32 [262144], replicated, may hold values from -6 to 6
- upper_bound: float32 [262144], replicated, may hold values from 0.5 to 2
Outputs:
- primal_final: float32 [262144], replicated
- dual_final: float32 [524288], P(('grp', 'dev'))
- weight_final: float32 [1], replicated
Inputs may be any that keep to these rules, and one draw needn't show every extreme that they name: `block_counts`: each device's 32 row blocks have 1 to 4 tiles each and 80 at most together; some device has exactly 80 in every draw. `destination`: on every device the 32 entries are each of 0 to 31 once.
All inputs are finite; a program needn't handle non-finite values.
Results may differ from a plain program's by a relative error of at most 0.0015.
Values may be sent and summed in bfloat16 or wider, within the bound.
A program may use at most 128 MiB of HBM per device.

v0:
```python
import jax
import jax.numpy as jnp
from jax import lax
from jax.sharding import Mesh
from jax.sharding import PartitionSpec as P

NCB = 256
ITERS = 3
GRP_DEV = ("grp", "dev_0", "dev_1", "dev_2")
DEV = ("dev_0", "dev_1", "dev_2")


step_scale = 0.3


def in_blocks(array, dim, length):
    before, after = (array.shape[:dim], array.shape[dim + 1 :])
    return jnp.moveaxis(array.reshape(*before, length, -1, *after), dim, 0)


def summed_on_arrival(array, axis, dim):
    length = lax.axis_size(axis)
    tiles = lax.all_to_all(in_blocks(array, dim, length), axis, 0, 0, tiled=True)
    return jnp.sum(tiles, axis=0)


def sum_by_axis(array, axes, dim):
    far, near = axes
    own = summed_on_arrival(in_blocks(array, dim, lax.axis_size(far)), near, dim + 1)
    return jnp.sum(lax.all_to_all(own, far, 0, 0, tiled=True), axis=0)


def copy_for_each(array, axis):
    length = lax.axis_size(axis)
    return lax.all_to_all(
        jnp.broadcast_to(array[None], (length, *array.shape)), axis, 0, 0, tiled=True
    )


def laid_out(tiles, dim):
    tiles = jnp.moveaxis(tiles, 0, dim)
    dims = tiles.shape
    return tiles.reshape(*dims[:dim], dims[dim] * dims[dim + 1], *dims[dim + 2 :])


def gathered_by_axis(array, axes, dim):
    far, near = axes
    tiles = copy_for_each(copy_for_each(array, far), near)
    return laid_out(tiles.swapaxes(0, 1).reshape(-1, *array.shape), dim)


def taken_together(array, axis):
    everything = copy_for_each(array, axis)
    return jnp.sum(everything, axis=0)


def by_axis(array, axes):
    far, near = axes
    nearer = taken_together(array, near)
    return taken_together(nearer, far)


def together(arrays, axis):
    ends = [0]
    for a in arrays:
        ends.append(ends[-1] + a.size)
    running = by_axis(jnp.concatenate([a.ravel() for a in arrays]), axis)
    return tuple((running[b:e].reshape(a.shape) for a, b, e in zip(arrays, ends, ends[1:])))


def row_products(tile_store, vector_bf, blocks):
    tile_set, tile_cols, owners, live_flags = tile_store
    vector_table = vector_bf.reshape(-1, tile_set.shape[2])
    column_hot = (
        tile_cols[:, None] == jnp.arange(vector_table.shape[0], dtype=jnp.int32)[None, :]
    ).astype(jnp.bfloat16)
    picked = jnp.dot(column_hot, vector_table, preferred_element_type=jnp.float32).astype(
        jnp.bfloat16
    )
    product = jnp.einsum("src,sc->sr", tile_set, picked, preferred_element_type=jnp.float32)
    product = jnp.where(live_flags[:, None], product, 0.0)
    owner_hot = (jnp.arange(blocks, dtype=jnp.int32)[:, None] == owners[None, :]).astype(
        jnp.float32
    )
    return jnp.dot(owner_hot, product, precision=lax.Precision.HIGHEST)


def column_products(tile_store, rows_bf):
    tile_set, tile_cols, owners, live_flags = tile_store
    blocks = rows_bf.shape[0]
    owner_hot = (owners[:, None] == jnp.arange(blocks, dtype=jnp.int32)[None, :]).astype(
        jnp.bfloat16
    )
    picked_rows = jnp.dot(owner_hot, rows_bf, preferred_element_type=jnp.float32).astype(
        jnp.bfloat16
    )
    product = jnp.einsum("src,sr->sc", tile_set, picked_rows, preferred_element_type=jnp.float32)
    product = jnp.where(live_flags[:, None], product, 0.0)
    column_hot = (jnp.arange(NCB, dtype=jnp.int32)[:, None] == tile_cols[None, :]).astype(
        jnp.float32
    )
    return jnp.dot(column_hot, product, precision=lax.Precision.HIGHEST).reshape(-1)


def per_device(
    matrix_tiles,
    tile_column,
    block_counts,
    destination,
    row_bounds,
    dual_start,
    primal_start,
    cost_vector,
    upper_bound,
):
    blocks = block_counts.shape[0]
    rows_per = matrix_tiles.shape[1]
    slot_count = matrix_tiles.shape[0]
    starts = jnp.cumsum(block_counts) - block_counts
    slot_ids = jnp.arange(slot_count, dtype=jnp.int32)
    owners = jnp.sum((starts[None, 1:] <= slot_ids[:, None]).astype(jnp.int32), axis=1)
    bounds_here = row_bounds.reshape(blocks, rows_per)
    dual_here = dual_start.reshape(blocks, rows_per)
    peer_ids = jnp.arange(blocks, dtype=jnp.int32)
    inverse = jnp.sum(
        jnp.where(destination[None, :] == peer_ids[:, None], peer_ids[None, :], 0), axis=1
    )
    tile_store = (matrix_tiles, tile_column, owners, slot_ids < jnp.sum(block_counts))
    bounds = bounds_here.astype(jnp.float32)
    dual_state = dual_here.astype(jnp.float32)
    primal = primal_start
    weight = jnp.ones((), jnp.float32)
    row_image = row_products(tile_store, primal.astype(jnp.bfloat16), blocks)
    for iteration in range(ITERS):
        step_primal = step_scale / weight
        step_dual = step_scale * weight
        partial_value = column_products(tile_store, dual_state.astype(jnp.bfloat16))
        column_share = sum_by_axis(partial_value, (("grp", "dev_0", "dev_1"), "dev_2"), 0)
        share_len = column_share.shape[0]
        share_start = lax.axis_index(GRP_DEV) * share_len
        primal_share = lax.dynamic_slice_in_dim(primal, share_start, share_len)
        cost_share = lax.dynamic_slice_in_dim(cost_vector, share_start, share_len)
        upper_share = lax.dynamic_slice_in_dim(upper_bound, share_start, share_len)
        new_share = jnp.clip(
            primal_share - step_primal * (cost_share - column_share), 0.0, upper_share
        )
        change_part = jnp.sum((new_share - primal_share) ** 2)
        primal_next = gathered_by_axis(new_share, (("grp", "dev_0", "dev_1"), "dev_2"), 0)
        next_image = row_products(tile_store, primal_next.astype(jnp.bfloat16), blocks)
        dual_state = jnp.maximum(
            dual_state + step_dual * (bounds - (2.0 * next_image - row_image)), 0.0
        )
        violation_part = jnp.sum(jnp.maximum(bounds - next_image, 0.0) ** 2)
        violation, change = together(
            (violation_part, change_part), (("grp", "dev_0", "dev_1"), "dev_2")
        )
        weight = jnp.sqrt(weight * jnp.sqrt((violation + 1e-06) / (change + 1e-06)))
        primal = primal_next
        row_image = next_image
    dual_final = lax.all_to_all(
        dual_state[inverse], DEV, split_axis=0, concat_axis=0, tiled=True
    ).reshape(-1)
    return (primal, dual_final, jnp.reshape(weight, (1,)))


def solution(mesh):
    split = Mesh(
        mesh.devices.reshape(mesh.shape["grp"], 4, 4, 2), ("grp", "dev_0", "dev_1", "dev_2")
    )
    return jax.shard_map(
        per_device,
        mesh=split,
        in_specs=(
            P(GRP_DEV, None, None),
            P(GRP_DEV),
            P(GRP_DEV),
            P(GRP_DEV),
            P(GRP_DEV),
            P(GRP_DEV),
            P(),
            P(),
            P(),
        ),
        out_specs=(P(), P(GRP_DEV), P()),
        check_vma=False,
    )
```

profile of v0, /device:TPU:0, one launch (start us, length us, event | category | flops | bytes accessed | tf_op | source)
XLA Modules:
  0.0 306.6 jit_solution(17771277475727326074)
XLA Ops:
  4.7 8.4 %fusion.38 = f32[80,1,1024]{2,1,0:T(1,128)S(1)} fusion(bf16[80,128,1024]{2,1,0:T(8,128)(2,1)} %param.9, bf16[80,128,1]{1,0,2:T(8,128)(2,1)S(1)} %fusion.4), kind=kOutput, calls=%fused_computation.61 | convolution fusion | flops 20971520 | bytes 21319680 | tf_op jit(solution)/shard_map/src,sr->sc/dot_general | solution.py:97
  15.1 4.6 %all_to_all.120 = f32[2,64,2048]{2,1,0:T(8,128)S(1)} all-to-all(f32[2,64,2048]{2,1,0:T(8,128)S(1)} %bitcast.120), channel_id=1, replica_groups=mesh['grp'=4,'dev_0'=4,'dev_1'=4,'dev_2'=2] {'dev_2'}, dimensions={0} | all-to-all | bytes 2097152 | tf_op jit(solution)/shard_map/all_to_all | solution.py:23
  21.0 11.5 %all-to-all-start.1 = ((f32[64,1,2048]{2,1,0:T(1,128)}), f32[64,1,2048]{2,1,0:T(1,128)S(1)}, u32[]{:S(2)}, u32[]{:S(2)}) async-start(f32[64,1,2048]{2,1,0:T(1,128)} %all_to_all.79), calls=%async_computation.1 | async-start | bytes 1048576 | tf_op jit(solution)/shard_map/all_to_all | solution.py:30
  33.1 13.0 %all-to-all-done.1 = f32[64,1,2048]{2,1,0:T(1,128)S(1)} async-done(((f32[64,1,2048]{2,1,0:T(1,128)}), f32[64,1,2048]{2,1,0:T(1,128)S(1)}, u32[]{:S(2)}, u32[]{:S(2)}) %all-to-all-start.1) | async-done | bytes 524320 | tf_op jit(solution)/shard_map/all_to_all | solution.py:30
  48.8 4.8 %all-to-all-start.2 = ((f32[64,1,2048]{2,1,0:T(1,128)}), f32[64,1,2048]{2,1,0:T(1,128)S(1)}, u32[]{:S(2)}, u32[]{:S(2)}) async-start(f32[64,1,2048]{2,1,0:T(1,128)} %broadcast_in_dim.88), calls=%async_computation.2 | async-start | bytes 1048576 | tf_op jit(solution)/shard_map/all_to_all | solution.py:35
  53.6 9.8 %fusion.20 = f32[80,1,128]{2,1,0:T(1,128)S(1)} fusion(bf16[80,128,1024]{2,1,0:T(8,128)(2,1)} %param.9, bf16[80,1024,1]{1,0,2:T(8,128)(2,1)S(1)} %fusion.1), kind=kOutput, calls=%fused_computation.41 | convolution fusion | flops 20971520 | bytes 21176320 | tf_op jit(solution)/shard_map/src,sc->sr/dot_general | solution.py:80
  66.0 4.6 %all_to_all.121 = f32[2,64,2048]{2,1,0:T(8,128)S(1)} all-to-all(f32[2,64,2048]{2,1,0:T(8,128)S(1)} %broadcast_in_dim.90), channel_id=1, replica_groups=mesh['grp'=4,'dev_0'=4,'dev_1'=4,'dev_2'=2] {'dev_2'}, dimensions={0} | all-to-all | bytes 2097152 | tf_op jit(solution)/shard_map/all_to_all | solution.py:35
  71.8 9.8 %fusion.22 = f32[80,1,128]{2,1,0:T(1,128)S(1)} fusion(bf16[80,128,1024]{2,1,0:T(8,128)(2,1)} %param.9, bf16[80,1024,1]{1,0,2:T(8,128)(2,1)S(1)} %fusion), kind=kOutput, calls=%fused_computation.43 | convolution fusion | flops 20971520 | bytes 21176320 | tf_op jit(solution)/shard_map/src,sc->sr/dot_general | solution.py:80
  88.2 8.4 %fusion.36 = f32[80,1,1024]{2,1,0:T(1,128)S(1)} fusion(bf16[80,128,1024]{2,1,0:T(8,128)(2,1)} %param.9, bf16[80,128,1]{1,0,2:T(8,128)(2,1)S(1)} %fusion.5), kind=kOutput, calls=%fused_computation.59 | convolution fusion | flops 20971520 | bytes 21319680 | tf_op jit(solution)/shard_map/src,sr->sc/dot_general | solution.py:97
  98.7 4.6 %all_to_all.123 = f32[2,64,2048]{2,1,0:T(8,128)S(1)} all-to-all(f32[2,64,2048]{2,1,0:T(8,128)S(1)} %bitcast.121), channel_id=1, replica_groups=mesh['grp'=4,'dev_0'=4,'dev_1'=4,'dev_2'=2] {'dev_2'}, dimensions={0} | all-to-all | bytes 2097152 | tf_op jit(solution)/shard_map/all_to_all | solution.py:23
  103.9 8.1 %all-to-all-start.5 = ((f32[64,1,2]{2,1,0:T(1,128)}), f32[64,1,2]{2,1,0:T(1,128)S(1)}, u32[]{:S(2)}, u32[]{:S(2)}) async-start(f32[64,1,2]{2,1,0:T(1,128)} %broadcast_in_dim.94), calls=%async_computation.5 | async-start | bytes 65536 | tf_op jit(solution)/shard_map/all_to_all | solution.py:35
  113.2 8.3 %all-to-all-done.5 = f32[64,1,2]{2,1,0:T(1,128)S(1)} async-done(((f32[64,1,2]{2,1,0:T(1,128)}), f32[64,1,2]{2,1,0:T(1,128)S(1)}, u32[]{:S(2)}, u32[]{:S(2)}) %all-to-all-start.5) | async-done | bytes 544 | tf_op jit(solution)/shard_map/all_to_all | solution.py:35
  121.5 5.0 %all-to-all-start.7 = ((f32[64,1,2048]{2,1,0:T(1,128)}), f32[64,1,2048]{2,1,0:T(1,128)S(1)}, u32[]{:S(2)}, u32[]{:S(2)}) async-start(f32[64,1,2048]{2,1,0:T(1,128)} %all_to_all.86), calls=%async_computation.7 | async-start | bytes 1048576 | tf_op jit(solution)/shard_map/all_to_all | solution.py:30
  129.5 9.1 %all-to-all-done.7 = f32[64,1,2048]{2,1,0:T(1,128)S(1)} async-done(((f32[64,1,2048]{2,1,0:T(1,128)}), f32[64,1,2048]{2,1,0:T(1,128)S(1)}, u32[]{:S(2)}, u32[]{:S(2)}) %all-to-all-start.7) | async-done | bytes 524320 | tf_op jit(solution)/shard_map/all_to_all | solution.py:30
  141.3 4.8 %all-to-all-start.8 = ((f32[64,1,2048]{2,1,0:T(1,128)}), f32[64,1,2048]{2,1,0:T(1,128)S(1)}, u32[]{:S(2)}, u32[]{:S(2)}) async-start(f32[64,1,2048]{2,1,0:T(1,128)} %broadcast_in_dim.95), calls=%async_computation.8 | async-start | bytes 1048576 | tf_op jit(solution)/shard_map/all_to_all | solution.py:35
  146.2 11.9 %all-to-all-done.8 = f32[64,1,2048]{2,1,0:T(1,128)S(1)} async-done(((f32[64,1,2048]{2,1,0:T(1,128)}), f32[64,1,2048]{2,1,0:T(1,128)S(1)}, u32[]{:S(2)}, u32[]{:S(2)}) %all-to-all-start.8) | async-done | bytes 524320 | tf_op jit(solution)/shard_map/all_to_all | solution.py:35
  158.3 4.6 %all_to_all.124 = f32[2,64,2048]{2,1,0:T(8,128)S(1)} all-to-all(f32[2,64,2048]{2,1,0:T(8,128)S(1)} %broadcast_in_dim.97), channel_id=1, replica_groups=mesh['grp'=4,'dev_0'=4,'dev_1'=4,'dev_2'=2] {'dev_2'}, dimensions={0} | all-to-all | bytes 2097152 | tf_op jit(solution)/shard_map/all_to_all | solution.py:35
  164.1 9.8 %fusion.17 = f32[80,1,128]{2,1,0:T(1,128)S(1)} fusion(bf16[80,128,1024]{2,1,0:T(8,128)(2,1)} %param.9, bf16[80,1024,1]{1,0,2:T(8,128)(2,1)S(1)} %fusion.2), kind=kOutput, calls=%fused_computation.38 | convolution fusion | flops 20971520 | bytes 21176320 | tf_op jit(solution)/shard_map/src,sc->sr/dot_general | solution.py:80
  176.1 13.7 %all_to_all.125 = f32[2,1,2]{2,1,0:T(1,128)S(1)} all-to-all(f32[2,1,2]{2,1,0:T(1,128)S(1)} %broadcast_in_dim.98), channel_id=1, replica_groups=mesh['grp'=4,'dev_0'=4,'dev_1'=4,'dev_2'=2] {'dev_2'}, dimensions={0} | all-to-all | bytes 32 | tf_op jit(solution)/shard_map/all_to_all | solution.py:35
  190.0 8.4 %fusion.34 = f32[80,1,1024]{2,1,0:T(1,128)S(1)} fusion(bf16[80,128,1024]{2,1,0:T(8,128)(2,1)} %param.9, bf16[80,128,1]{1,0,2:T(8,128)(2,1)S(1)} %fusion.6), kind=kOutput, calls=%fused_computation.57 | convolution fusion | flops 20971520 | bytes 21319680 | tf_op jit(solution)/shard_map/src,sr->sc/dot_general | solution.py:97
  200.5 4.6 %all_to_all.126 = f32[2,64,2048]{2,1,0:T(8,128)S(1)} all-to-all(f32[2,64,2048]{2,1,0:T(8,128)S(1)} %bitcast.123), channel_id=1, replica_groups=mesh['grp'=4,'dev_0'=4,'dev_1'=4,'dev_2'=2] {'dev_2'}, dimensions={0} | all-to-all | bytes 2097152 | tf_op jit(solution)/shard_map/all_to_all | solution.py:23
  205.7 4.8 %all-to-all-start.11 = ((f32[64,1,2]{2,1,0:T(1,128)}), f32[64,1,2]{2,1,0:T(1,128)S(1)}, u32[]{:S(2)}, u32[]{:S(2)}) async-start(f32[64,1,2]{2,1,0:T(1,128)} %broadcast_in_dim.99), calls=%async_computation.11 | async-start | bytes 65536 | tf_op jit(solution)/shard_map/all_to_all | solution.py:35
  211.8 8.3 %all-to-all-done.11 = f32[64,1,2]{2,1,0:T(1,128)S(1)} async-done(((f32[64,1,2]{2,1,0:T(1,128)}), f32[64,1,2]{2,1,0:T(1,128)S(1)}, u32[]{:S(2)}, u32[]{:S(2)}) %all-to-all-start.11) | async-done | bytes 544 | tf_op jit(solution)/shard_map/all_to_all | solution.py:35
  220.1 5.0 %all-to-all-start.13 = ((f32[64,1,2048]{2,1,0:T(1,128)}), f32[64,1,2048]{2,1,0:T(1,128)S(1)}, u32[]{:S(2)}, u32[]{:S(2)}) async-start(f32[64,1,2048]{2,1,0:T(1,128)} %all_to_all.93), calls=%async_computation.13 | async-start | bytes 1048576 | tf_op jit(solution)/shard_map/all_to_all | solution.py:30
  228.1 9.2 %all-to-all-done.13 = f32[64,1,2048]{2,1,0:T(1,128)S(1)} async-done(((f32[64,1,2048]{2,1,0:T(1,128)}), f32[64,1,2048]{2,1,0:T(1,128)S(1)}, u32[]{:S(2)}, u32[]{:S(2)}) %all-to-all-start.13) | async-done | bytes 524320 | tf_op jit(solution)/shard_map/all_to_all | solution.py:30
  240.0 4.8 %all-to-all-start.14 = ((f32[64,1,2048]{2,1,0:T(1,128)}), f32[64,1,2048]{2,1,0:T(1,128)S(1)}, u32[]{:S(2)}, u32[]{:S(2)}) async-start(f32[64,1,2048]{2,1,0:T(1,128)} %broadcast_in_dim.100), calls=%async_computation.14 | async-start | bytes 1048576 | tf_op jit(solution)/shard_map/all_to_all | solution.py:35
  245.0 11.7 %all-to-all-done.14 = f32[64,1,2048]{2,1,0:T(1,128)S(1)} async-done(((f32[64,1,2048]{2,1,0:T(1,128)}), f32[64,1,2048]{2,1,0:T(1,128)S(1)}, u32[]{:S(2)}, u32[]{:S(2)}) %all-to-all-start.14) | async-done | bytes 524320 | tf_op jit(solution)/shard_map/all_to_all | solution.py:35
  257.0 4.6 %all_to_all.127 = f32[2,64,2048]{2,1,0:T(8,128)S(1)} all-to-all(f32[2,64,2048]{2,1,0:T(8,128)S(1)} %broadcast_in_dim.102), channel_id=1, replica_groups=mesh['grp'=4,'dev_0'=4,'dev_1'=4,'dev_2'=2] {'dev_2'}, dimensions={0} | all-to-all | bytes 2097152 | tf_op jit(solution)/shard_map/all_to_all | solution.py:35
  262.8 9.8 %fusion.14 = f32[80,1,128]{2,1,0:T(1,128)S(1)} fusion(bf16[80,128,1024]{2,1,0:T(8,128)(2,1)} %param.9, bf16[80,1024,1]{1,0,2:T(8,128)(2,1)S(1)} %fusion.3), kind=kOutput, calls=%fused_computation.35 | convolution fusion | flops 20971520 | bytes 21176320 | tf_op jit(solution)/shard_map/src,sc->sr/dot_general | solution.py:80
  279.1 4.8 %all-to-all-start.18 = ((f32[64,1,2]{2,1,0:T(1,128)}), f32[64,1,2]{2,1,0:T(1,128)S(1)}, u32[]{:S(2)}, u32[]{:S(2)}) async-start(f32[64,1,2]{2,1,0:T(1,128)} %broadcast_in_dim.106), calls=%async_computation.18 | async-start | bytes 65536 | tf_op jit(solution)/shard_map/all_to_all | solution.py:35
  287.0 6.5 %all-to-all-done.18 = f32[64,1,2]{2,1,0:T(1,128)S(1)} async-done(((f32[64,1,2]{2,1,0:T(1,128)}), f32[64,1,2]{2,1,0:T(1,128)S(1)}, u32[]{:S(2)}, u32[]{:S(2)}) %all-to-all-start.18) | async-done | bytes 544 | tf_op jit(solution)/shard_map/all_to_all | solution.py:35
  299.5 5.2 %all-to-all-done.16 = f32[32,1,128]{2,1,0:T(1,128)S(1)} async-done(((f32[32,1,128]{2,1,0:T(1,128)}), f32[32,1,128]{2,1,0:T(1,128)S(1)}, u32[]{:S(2)}, u32[]{:S(2)}) %all-to-all-start.16) | async-done | bytes 16416 | tf_op jit(solution)/shard_map/all_to_all | solution.py:160
  (102 shorter events, 57.2 us)
Async XLA Ops:
  0.6 12.5 %copy-start.2 = (s32[80]{0:T(128)S(1)}, s32[80]{0:T(128)}, u32[]{:S(2)}) copy-start(s32[80]{0:T(128)} %param.10) | copy-start | bytes 964
  0.6 31.9 %copy-start = (f32[262144]{0:T(1024)S(1)}, f32[262144]{0:T(1024)}, u32[]{:S(2)}) copy-start(f32[262144]{0:T(1024)} %param.15) | copy-start | bytes 3145732
  21.0 25.1 %all-to-all-start.1 = ((f32[64,1,2048]{2,1,0:T(1,128)}), f32[64,1,2048]{2,1,0:T(1,128)S(1)}, u32[]{:S(2)}, u32[]{:S(2)}) async-start(f32[64,1,2048]{2,1,0:T(1,128)} %all_to_all.79), calls=%async_computation.1 | async-start | bytes 1048576 | tf_op jit(solution)/shard_map/all_to_all | solution.py:30
  48.8 16.9 %all-to-all-start.2 = ((f32[64,1,2048]{2,1,0:T(1,128)}), f32[64,1,2048]{2,1,0:T(1,128)S(1)}, u32[]{:S(2)}, u32[]{:S(2)}) async-start(f32[64,1,2048]{2,1,0:T(1,128)} %broadcast_in_dim.88), calls=%async_computation.2 | async-start | bytes 1048576 | tf_op jit(solution)/shard_map/all_to_all | solution.py:35
  70.7 11.0 %copy-start.1 = (bf16[4096]{0:T(1024)(128)(2,1)S(1)}, bf16[4096]{0:T(1024)(128)(2,1)}, u32[]{:S(2)}) copy-start(bf16[4096]{0:T(1024)(128)(2,1)} %param.13) | copy-start | bytes 24580
  70.7 17.1 %copy-start.3 = (bf16[4096]{0:T(1024)(128)(2,1)S(1)}, bf16[4096]{0:T(1024)(128)(2,1)}, u32[]{:S(2)}) copy-start(bf16[4096]{0:T(1024)(128)(2,1)} %param.14) | copy-start | bytes 24580
  103.9 17.6 %all-to-all-start.5 = ((f32[64,1,2]{2,1,0:T(1,128)}), f32[64,1,2]{2,1,0:T(1,128)S(1)}, u32[]{:S(2)}, u32[]{:S(2)}) async-start(f32[64,1,2]{2,1,0:T(1,128)} %broadcast_in_dim.94), calls=%async_computation.5 | async-start | bytes 65536 | tf_op jit(solution)/shard_map/all_to_all | solution.py:35
  121.5 17.1 %all-to-all-start.7 = ((f32[64,1,2048]{2,1,0:T(1,128)}), f32[64,1,2048]{2,1,0:T(1,128)S(1)}, u32[]{:S(2)}, u32[]{:S(2)}) async-start(f32[64,1,2048]{2,1,0:T(1,128)} %all_to_all.86), calls=%async_computation.7 | async-start | bytes 1048576 | tf_op jit(solution)/shard_map/all_to_all | solution.py:30
  141.3 16.7 %all-to-all-start.8 = ((f32[64,1,2048]{2,1,0:T(1,128)}), f32[64,1,2048]{2,1,0:T(1,128)S(1)}, u32[]{:S(2)}, u32[]{:S(2)}) async-start(f32[64,1,2048]{2,1,0:T(1,128)} %broadcast_in_dim.95), calls=%async_computation.8 | async-start | bytes 1048576 | tf_op jit(solution)/shard_map/all_to_all | solution.py:35
  190.0 54.8 %copy-start.4 = (s32[32]{0:T(128)S(1)}, s32[32]{0:T(128)}, u32[]{:S(2)}) copy-start(s32[32]{0:T(128)} %param.12) | copy-start | bytes 388
  205.7 14.4 %all-to-all-start.11 = ((f32[64,1,2]{2,1,0:T(1,128)}), f32[64,1,2]{2,1,0:T(1,128)S(1)}, u32[]{:S(2)}, u32[]{:S(2)}) async-start(f32[64,1,2]{2,1,0:T(1,128)} %broadcast_in_dim.99), calls=%async_computation.11 | async-start | bytes 65536 | tf_op jit(solution)/shard_map/all_to_all | solution.py:35
  220.1 17.2 %all-to-all-start.13 = ((f32[64,1,2048]{2,1,0:T(1,128)}), f32[64,1,2048]{2,1,0:T(1,128)S(1)}, u32[]{:S(2)}, u32[]{:S(2)}) async-start(f32[64,1,2048]{2,1,0:T(1,128)} %all_to_all.93), calls=%async_computation.13 | async-start | bytes 1048576 | tf_op jit(solution)/shard_map/all_to_all | solution.py:30
  240.0 16.7 %all-to-all-start.14 = ((f32[64,1,2048]{2,1,0:T(1,128)}), f32[64,1,2048]{2,1,0:T(1,128)S(1)}, u32[]{:S(2)}, u32[]{:S(2)}) async-start(f32[64,1,2048]{2,1,0:T(1,128)} %broadcast_in_dim.100), calls=%async_computation.14 | async-start | bytes 1048576 | tf_op jit(solution)/shard_map/all_to_all | solution.py:35
  279.1 14.4 %all-to-all-start.18 = ((f32[64,1,2]{2,1,0:T(1,128)}), f32[64,1,2]{2,1,0:T(1,128)S(1)}, u32[]{:S(2)}, u32[]{:S(2)}) async-start(f32[64,1,2]{2,1,0:T(1,128)} %broadcast_in_dim.106), calls=%async_computation.18 | async-start | bytes 65536 | tf_op jit(solution)/shard_map/all_to_all | solution.py:35
  293.5 11.2 %all-to-all-start.16 = ((f32[32,1,128]{2,1,0:T(1,128)}), f32[32,1,128]{2,1,0:T(1,128)S(1)}, u32[]{:S(2)}, u32[]{:S(2)}) async-start(f32[32,1,128]{2,1,0:T(1,128)} %bitcast.41), calls=%async_computation.16 | async-start | bytes 32768 | tf_op jit(solution)/shard_map/all_to_all | solution.py:160
where the time goes:
time: 312 us; the launch traced here: 307 us
  waiting for transfers between devices  85.5 us (27%)
  matrix products  71.7 us (23%)
  starting transfers between devices  57.4 us (18%)
  blocking collectives  48.7 us (16%)
  local copies, waits for them, and re-layouts  24.1 us (8%)
  other arithmetic  12.3 us (4%)
  between operations  6.81 us (2%)
    all_to_all x6, waiting for transfers between devices, copy_for_each(): lax.all_to_all(jnp.broadcast_to(array[None], (length, *array.shape)), axi...  49 us
    dot_general x4, matrix products, row_products(): jnp.einsum('src,sc->sr', tile_set, picked, preferred_element_type=jnp.flo...  39.3 us
    all_to_all x6, blocking collectives, copy_for_each(): lax.all_to_all(jnp.broadcast_to(array[None], (length, *array.shape)), axi...  35 us
    all_to_all x6, starting transfers between devices, copy_for_each(): lax.all_to_all(jnp.broadcast_to(array[None], (length, *array.shape)), axi...  32.1 us
    all_to_all x3, waiting for transfers between devices, sum_by_axis(): return jnp.sum(lax.all_to_all(own, far, 0, 0, tiled=True), axis=0)  31.3 us
    dot_general x3, matrix products, column_products(): jnp.einsum('src,sr->sc', tile_set, picked_rows, preferred_element_type=jn...  25.3 us
    all_to_all x3, starting transfers between devices, sum_by_axis(): return jnp.sum(lax.all_to_all(own, far, 0, 0, tiled=True), axis=0)  21.5 us
    all_to_all x3, blocking collectives, summed_on_arrival(): lax.all_to_all(in_blocks(array, dim, length), axis, 0, 0, tiled=True)  13.7 us
  transfers between devices with their start and end apart: 10, of which 10 were waited for; matrix products, arithmetic and copies ran while one was open for 6% of the time, Pallas kernels for 0%

commit v1 on v0

v1 whole, which is shorter than its diff:
```python
import jax
import jax.numpy as jnp
from jax import lax
from jax.experimental import pallas as pl
from jax.experimental.pallas import tpu as pltpu
from jax.sharding import PartitionSpec as P

MESH = pl.DeviceIdType.MESH
GRP_DEV = ("grp", "dev")

NCB = 256
CB = 1024
TR = 128
SLOTS = 80
BLOCKS = 32
ITERS = 3
CH = 4
LANES = CB // CH
GROUP = 16
NG = SLOTS // GROUP
PLANE = 32
ZN = 4
STEP = 0.3

F32 = jnp.float32
BF16 = jnp.bfloat16


def iota(shape, dim):
    return lax.broadcasted_iota(jnp.int32, shape, dim)


def dot(a, b, dims=((1,), (0,)), exact=False):
    return lax.dot_general(
        a,
        b,
        (dims, ((), ())),
        precision=lax.Precision.HIGHEST if exact else None,
        preferred_element_type=F32,
    )


def kernel(
    tiles_hbm,
    col_ref,
    cnt_ref,
    dst_ref,
    bnd_ref,
    dual0_ref,
    x_hbm,
    c_hbm,
    u_hbm,
    xo_ref,
    do_ref,
    wo_ref,
    tiles,
    x,
    cost,
    upper,
    xtab,
    cmat,
    ctmat,
    omat,
    otmat,
    bd,
    prod,
    macc,
    vsel,
    img,
    dual,
    wgt,
    snd,
    rcv,
    zsnd,
    zrcv,
    grad,
    vsnd,
    vrcv,
    vzsnd,
    vzrcv,
    dsnd,
    drcv,
    bounds,
    tile_sem,
    vec_sem,
    out_sem,
    snd_sem,
    rcv_sem,
    zsnd_sem,
    zrcv_sem,
    gzs_sem,
    gzr_sem,
    gs_sem,
    gr_sem,
    vs_sem,
    vr_sem,
    vzs_sem,
    vzr_sem,
    ds_sem,
    dr_sem,
):
    z = lax.axis_index("grp")
    me = lax.axis_index("dev")

    vec_copies = [
        pltpu.make_async_copy(h, v, vec_sem.at[n])
        for n, (h, v) in enumerate(((x_hbm, x), (c_hbm, cost), (u_hbm, upper)))
    ]
    vec_copies[0].start()

    def tile_copy(j):
        return pltpu.make_async_copy(
            tiles_hbm.at[:, :, pl.ds(LANES * j, LANES)], tiles.at[j], tile_sem.at[j]
        )

    for j in range(CH):
        tile_copy(j).start()
    vec_copies[1].start()
    vec_copies[2].start()

    barrier = pltpu.get_barrier_semaphore()

    def greet(k, _):
        pl.semaphore_signal(
            barrier, inc=1, device_id=(z, lax.rem(me + k, PLANE)), device_id_type=MESH
        )
        return 0

    lax.fori_loop(1, PLANE, greet, 0)
    for k in range(1, ZN):
        pl.semaphore_signal(
            barrier, inc=1, device_id=(lax.rem(z + k, ZN), me), device_id_type=MESH
        )

    def to_plane(src, dst, ssem, rsem):
        def go(k, _):
            peer = lax.rem(me + k, PLANE)
            pltpu.make_async_remote_copy(
                src_ref=src(peer),
                dst_ref=dst,
                send_sem=ssem,
                recv_sem=rsem,
                device_id=(z, peer),
                device_id_type=MESH,
            ).start()
            return 0

        lax.fori_loop(1, PLANE, go, 0)

    def to_z(src, dst, ssem, rsem, peer_z):
        pltpu.make_async_remote_copy(
            src_ref=src,
            dst_ref=dst,
            send_sem=ssem,
            recv_sem=rsem,
            device_id=(peer_z, me),
            device_id_type=MESH,
        ).start()

    def await_bytes(ref, sem):
        pltpu.make_async_copy(ref, ref, sem).wait()

    cols = jnp.broadcast_to(col_ref[...], (NCB, SLOTS))
    onehot = (cols == iota((NCB, SLOTS), 0)).astype(F32)
    onehot = jnp.concatenate([onehot, jnp.zeros((NCB, TR - SLOTS), F32)], axis=1)
    cmat[...] = onehot.astype(BF16)
    ctmat[...] = onehot.T.astype(BF16)
    counts = jnp.broadcast_to(cnt_ref[...], (TR, BLOCKS)).astype(F32)
    below = (iota((BLOCKS, BLOCKS), 1) < iota((BLOCKS, BLOCKS), 0)).astype(F32)
    upto = (iota((BLOCKS, BLOCKS), 1) <= iota((BLOCKS, BLOCKS), 0)).astype(F32)
    starts = dot(below, counts, ((1,), (1,)))
    ends = dot(upto, counts, ((1,), (1,)))
    slot = iota((BLOCKS, TR), 1).astype(F32)
    owner = jnp.where((starts <= slot) & (slot < ends), 1.0, 0.0)
    omat[...] = owner
    owner = jnp.concatenate([owner, jnp.zeros((TR - BLOCKS, TR), F32)], axis=0)
    otmat[...] = owner.T.astype(BF16)
    prod[...] = jnp.zeros_like(prod)
    macc[...] = jnp.zeros_like(macc)
    wgt[...] = jnp.ones_like(wgt)
    dual[...] = jnp.zeros_like(dual)
    dual[pl.ds(0, BLOCKS), :] = dual0_ref[...].astype(F32)
    bounds[...] = bnd_ref[...].astype(F32)

    def pieces(j, body, start):
        def row(p, carry):
            for c in range(2):
                at = pl.ds(TR * p + 2 * j + c, 16, stride=8)
                carry = body(p, c, at, carry)
            return carry

        return lax.fori_loop(0, 16, row, start)

    def table(j, p, c, value):
        xtab[j, pl.ds(pl.multiple_of(16 * p, 16), 16), pl.ds(TR * c, TR)] = value.astype(BF16)

    vec_copies[0].wait()
    for j in range(CH):

        def first_table(p, c, at, carry, j=j):
            table(j, p, c, x[at, :])
            return carry

        pieces(j, first_table, 0)

    def columns(it, j):
        def group(g, _):
            rows = pl.ds(pl.multiple_of(GROUP * g, GROUP), GROUP)
            block = tiles[j, rows].reshape(GROUP * TR, LANES)
            prod[rows, :] = dot(bd[g], block)
            return 0

        lax.fori_loop(0, NG, group, 0)
        full = prod[...]
        high = full.astype(BF16)
        low = (full - high.astype(F32)).astype(BF16)
        total = dot(cmat[...], high) + dot(cmat[...], low)
        total = total.astype(BF16)
        for c in range(2):
            snd[it, j, pl.ds(16 * c, 16)] = total[:, TR * c : TR * (c + 1)].reshape(16, 16, TR)
        to_plane(lambda i: snd.at[it, j, i], rcv.at[it, j, me], snd_sem.at[it, j], rcv_sem.at[it, j])

    def rows(j):
        vsel[...] = dot(ctmat[...], xtab[j]).astype(BF16)
        lane = iota((TR, TR), 1)

        def group(g, merged):
            at = pl.ds(pl.multiple_of(GROUP * g, GROUP), GROUP)
            block = tiles[j, at].reshape(GROUP * TR, LANES)
            out = dot(block, vsel[...], ((1,), (1,)))
            for k in range(GROUP):
                merged = jnp.where(lane == GROUP * g + k, out[TR * k : TR * (k + 1)], merged)
            return merged

        macc[...] += lax.fori_loop(0, NG, group, jnp.zeros((TR, TR), F32))

    def rows_done():
        out = dot(omat[...], macc[...], ((1,), (1,)), exact=True)
        macc[...] = jnp.zeros_like(macc)
        return out

    def plane_sum(it, j):
        rcv[it, j, me] = snd[it, j, me]
        await_bytes(rcv.at[it, j, pl.ds(0, PLANE - 1)], rcv_sem.at[it, j])
        total = rcv[it, j, 0].astype(F32)
        for i in range(1, PLANE):
            total += rcv[it, j, i].astype(F32)

        @pl.when(z == j)
        def _():
            zrcv[it, j] = total

        @pl.when(z != j)
        def _():
            zsnd[it, j] = total
            to_z(zsnd.at[it, j], zrcv.at[it, z], zsnd_sem.at[it, j], zrcv_sem.at[it], j)

    def root_sum(it, j):
        @pl.when(z == j)
        def _():
            await_bytes(zrcv.at[it, pl.ds(0, ZN - 1)], zrcv_sem.at[it])
            total = zrcv[it, 0] + zrcv[it, 1] + zrcv[it, 2] + zrcv[it, 3]
            grad[it, j, me] = total.astype(BF16)
            for k in range(1, ZN):
                to_z(
                    grad.at[it, j, me],
                    grad.at[it, j, me],
                    gzs_sem.at[it],
                    gzr_sem.at[it, j],
                    lax.rem(z + k, ZN),
                )

    def spread(it, j):
        @pl.when(z != j)
        def _():
            await_bytes(grad.at[it, j, me], gzr_sem.at[it, j])

        to_plane(
            lambda i: grad.at[it, j, me], grad.at[it, j, me], gs_sem.at[it, j], gr_sem.at[it, j]
        )

    def violation_out(it, violated):
        part = violated[0:8] + violated[8:16] + violated[16:24] + violated[24:32]
        part = jnp.sum(part, axis=0, keepdims=True)
        vsnd[it] = part
        vrcv[it, me] = part
        to_plane(lambda i: vsnd.at[it], vrcv.at[it, me], vs_sem.at[it], vr_sem.at[it])

    def violation_plane(it):
        await_bytes(vrcv.at[it, pl.ds(0, PLANE - 1)], vr_sem.at[it])
        total = vrcv[it, 0]
        for i in range(1, PLANE):
            total += vrcv[it, i]
        vzsnd[it] = total
        vzrcv[it, z] = total
        for k in range(1, ZN):
            to_z(
                vzsnd.at[it],
                vzrcv.at[it, z],
                vzs_sem.at[it],
                vzr_sem.at[it],
                lax.rem(z + k, ZN),
            )

    def new_weight(it):
        await_bytes(vzrcv.at[it, pl.ds(0, ZN - 1)], vzr_sem.at[it])
        total = vzrcv[it, 0] + vzrcv[it, 1] + vzrcv[it, 2] + vzrcv[it, 3]
        violation = jnp.sum(total, axis=1, keepdims=True)
        change = wgt[pl.ds(8, 8), :]
        ratio = (jnp.broadcast_to(violation, (8, TR)) + 1e-6) / (change + 1e-6)
        wgt[pl.ds(0, 8), :] = jnp.sqrt(wgt[pl.ds(0, 8), :] * jnp.sqrt(ratio))

    def update(it, j, tau, moved):
        def piece(p, c, at, carry):
            old = x[at, :]
            slope = grad[it, j, 16 * c + p].astype(F32)
            new = jnp.minimum(jnp.maximum(old - tau * (cost[at, :] - slope), 0.0), upper[at, :])
            x[at, :] = new
            table(j, p, c, new)
            return carry + (new - old) * (new - old)

        return pieces(j, piece, moved)

    def iteration(it, _):
        chosen = dot(otmat[...], dual[...].astype(BF16))
        line = iota((GROUP, TR), 0)
        for g in range(NG):
            part = chosen[GROUP * g : GROUP * (g + 1)]
            for k in range(GROUP):
                bd[g, :, pl.ds(TR * k, TR)] = jnp.where(line == k, part, 0.0).astype(BF16)
        for j in range(CH):

            @pl.when(it == 0)
            def _():
                tile_copy(j).wait()
                if j == 0:
                    pl.semaphore_wait(barrier, PLANE - 1 + ZN - 1)

            columns(it, j)

        def early_rows(j):
            @pl.when(it == 0)
            def _():
                rows(j)

        plane_sum(it, 0)
        plane_sum(it, 1)
        root_sum(it, 0)
        plane_sum(it, 2)
        root_sum(it, 1)
        plane_sum(it, 3)
        early_rows(0)
        spread(it, 0)
        root_sum(it, 2)
        spread(it, 1)
        root_sum(it, 3)
        early_rows(1)

        @pl.when(it > 0)
        def _():
            violation_plane(it - 1)

        spread(it, 2)
        spread(it, 3)
        early_rows(2)
        early_rows(3)

        @pl.when(it == 0)
        def _():
            img[...] = rows_done()
            vec_copies[1].wait()
            vec_copies[2].wait()

        @pl.when(it > 0)
        def _():
            new_weight(it - 1)

        weight = wgt[pl.ds(0, 1), :]
        tau = STEP / weight
        sigma = STEP * weight
        moved = jnp.zeros((16, TR), F32)
        for j in range(CH):
            grad_at = grad.at[it, j, pl.ds(0, PLANE - 1)]
            await_bytes(grad_at, gr_sem.at[it, j])
            moved = update(it, j, tau, moved)
            rows(j)

        @pl.when(it == ITERS - 1)
        def _():
            pltpu.make_async_copy(x, xo_ref, out_sem).start()

        change = jnp.sum(jnp.sum(moved, axis=0, keepdims=True), axis=1, keepdims=True)
        wgt[pl.ds(8, 8), :] = jnp.broadcast_to(change, (8, TR))
        image = rows_done()
        violated = jnp.maximum(bounds[...] - image, 0.0)
        violation_out(it, violated * violated)
        dual[pl.ds(0, BLOCKS), :] = jnp.maximum(
            dual[pl.ds(0, BLOCKS), :] + sigma * (bounds[...] - (2.0 * image - img[...])), 0.0
        )
        img[...] = image
        return 0

    lax.fori_loop(0, ITERS, iteration, 0)

    hot = jnp.broadcast_to(dst_ref[...], (BLOCKS, BLOCKS)) == iota((BLOCKS, BLOCKS), 0)
    ordered = dot(hot.astype(F32), dual[pl.ds(0, BLOCKS), :], exact=True)
    for i in range(BLOCKS):
        dsnd[i] = ordered[i : i + 1]
    drcv[me] = dsnd[me]
    to_plane(lambda i: dsnd.at[i], drcv.at[me], ds_sem, dr_sem)
    violation_plane(ITERS - 1)
    await_bytes(drcv.at[pl.ds(0, PLANE - 1)], dr_sem)
    do_ref[...] = drcv[...]
    new_weight(ITERS - 1)
    wo_ref[...] = wgt[pl.ds(0, 8), :]

    def drain(it, _):
        for j in range(CH):
            await_bytes(snd.at[it, j, pl.ds(0, PLANE - 1)], snd_sem.at[it, j])
            await_bytes(grad.at[it, j, pl.ds(0, PLANE - 1)], gs_sem.at[it, j])

            @pl.when(z != j)
            def _():
                await_bytes(zsnd.at[it, j], zsnd_sem.at[it, j])

        await_bytes(grad.at[it, 0, pl.ds(0, ZN - 1)], gzs_sem.at[it])
        await_bytes(vrcv.at[it, pl.ds(0, PLANE - 1)], vs_sem.at[it])
        await_bytes(vzrcv.at[it, pl.ds(0, ZN - 1)], vzs_sem.at[it])
        return 0

    lax.fori_loop(0, ITERS, drain, 0)
    await_bytes(dsnd.at[pl.ds(0, PLANE - 1)], ds_sem)
    pltpu.make_async_copy(x, xo_ref, out_sem).wait()


def per_device(tiles, col, counts, dest, bounds, dual0, primal, cost, upper):
    anywhere = pl.BlockSpec(memory_space=pl.ANY)
    vmem = pl.BlockSpec(memory_space=pltpu.VMEM)
    dma = pltpu.SemaphoreType.DMA
    flat = (NCB * CB // TR, TR)
    x_out, dual_out, weight = pl.pallas_call(
        kernel,
        out_shape=(
            jax.ShapeDtypeStruct(flat, F32),
            jax.ShapeDtypeStruct((BLOCKS, 1, TR), F32),
            jax.ShapeDtypeStruct((8, TR), F32),
        ),
        in_specs=[anywhere, vmem, vmem, vmem, vmem, vmem, anywhere, anywhere, anywhere],
        out_specs=(anywhere, vmem, vmem),
        scratch_shapes=[
            pltpu.VMEM((CH, SLOTS, TR, LANES), BF16),
            pltpu.VMEM(flat, F32),
            pltpu.VMEM(flat, F32),
            pltpu.VMEM(flat, F32),
            pltpu.VMEM((CH, NCB, LANES), BF16),
            pltpu.VMEM((NCB, TR), BF16),
            pltpu.VMEM((TR, NCB), BF16),
            pltpu.VMEM((BLOCKS, TR), F32),
            pltpu.VMEM((TR, TR), BF16),
            pltpu.VMEM((NG, GROUP, GROUP * TR), BF16),
            pltpu.VMEM((TR, LANES), F32),
            pltpu.VMEM((TR, TR), F32),
            pltpu.VMEM((TR, LANES), BF16),
            pltpu.VMEM((BLOCKS, TR), F32),
            pltpu.VMEM((TR, TR), F32),
            pltpu.VMEM((16, TR), F32),
            pltpu.VMEM((ITERS, CH, PLANE, 16, TR), BF16),
            pltpu.VMEM((ITERS, CH, PLANE, 16, TR), BF16),
            pltpu.VMEM((ITERS, CH, 16, TR), F32),
            pltpu.VMEM((ITERS, ZN, 16, TR), F32),
            pltpu.VMEM((ITERS, CH, PLANE, 16, TR), BF16),
            pltpu.VMEM((ITERS, 1, TR), F32),
            pltpu.VMEM((ITERS, PLANE, 1, TR), F32),
            pltpu.VMEM((ITERS, 1, TR), F32),
            pltpu.VMEM((ITERS, ZN, 1, TR), F32),
            pltpu.VMEM((BLOCKS, 1, TR), F32),
            pltpu.VMEM((BLOCKS, 1, TR), F32),
            pltpu.VMEM((BLOCKS, TR), F32),
            dma((CH,)),
            dma((3,)),
            dma,
            dma((ITERS, CH)),
            dma((ITERS, CH)),
            dma((ITERS, CH)),
            dma((ITERS,)),
            dma((ITERS,)),
            dma((ITERS, CH)),
            dma((ITERS, CH)),
            dma((ITERS, CH)),
            dma((ITERS,)),
            dma((ITERS,)),
            dma((ITERS,)),
            dma((ITERS,)),
            dma,
            dma,
        ],
        compiler_params=pltpu.CompilerParams(
            collective_id=0, has_side_effects=True, vmem_limit_bytes=60 * 1024 * 1024
        ),
    )(
        tiles,
        col.reshape(1, SLOTS),
        counts.reshape(1, BLOCKS),
        dest.reshape(1, BLOCKS),
        bounds.reshape(BLOCKS, TR),
        dual0.reshape(BLOCKS, TR),
        primal.reshape(flat),
        cost.reshape(flat),
        upper.reshape(flat),
    )
    return x_out.reshape(-1), dual_out.reshape(-1), weight[0, :1]


def solution(mesh):
    split, whole = P(GRP_DEV), P()
    return jax.shard_map(
        per_device,
        mesh=mesh,
        in_specs=(P(GRP_DEV, None, None), split, split, split, split, split, whole, whole, whole),
        out_specs=(whole, split, whole),
        check_vma=False,
    )
```

time: 312 us -> 121 us (0.39); the launches traced: 307 us -> 121 us
  Pallas kernels: 0 us -> 115 us
  waiting for transfers between devices: 85.5 us -> 0 us
  matrix products: 71.7 us -> 0 us
  starting transfers between devices: 57.4 us -> 0 us
  blocking collectives: 48.7 us -> 0 us
  local copies, waits for them, and re-layouts: 24.1 us -> 4.77 us
  other arithmetic: 12.3 us -> 0 us
  between operations: 6.81 us -> 0.64 us
    pallas_call x0 -> x1, Pallas kernels: none -> 115 us  [per_device(): pl.pallas_call(kernel, out_shape=(jax.ShapeDtypeStruct(flat, F32), jax.Sh...]
    all_to_all x10 -> x0, waiting for transfers between devices: 85.5 us -> none  [the longest x6 49 us: copy_for_each(): lax.all_to_all(jnp.broadcast_to(array[None], (length, *array.shape)), axi...]
    dot_general x21 -> x0, matrix products: 71.7 us -> none  [the longest x4 39.3 us: row_products(): jnp.einsum('src,sc->sr', tile_set, picked, preferred_element_type=jnp.flo...]
    all_to_all x10 -> x0, starting transfers between devices: 57.4 us -> none  [the longest x6 32.1 us: copy_for_each(): lax.all_to_all(jnp.broadcast_to(array[None], (length, *array.shape)), axi...]
    all_to_all x9 -> x0, blocking collectives: 48.7 us -> none  [the longest x6 35 us: copy_for_each(): lax.all_to_all(jnp.broadcast_to(array[None], (length, *array.shape)), axi...]
    reduce_sum x18 -> x0, other arithmetic: 7.11 us -> none  [the longest x3 3.99 us: per_device(): change_part = jnp.sum((new_share - primal_share) ** 2)]
    broadcast_in_dim x12 -> x0, local copies, waits for them, and re-layouts: 5.36 us -> none  [copy_for_each(): jnp.broadcast_to(array[None], (length, *array.shape))]
    another operation x7 -> x0, local copies, waits for them, and re-layouts: 4.74 us -> none  [the longest x6 3.91 us: in_blocks(): return jnp.moveaxis(array.reshape(*before, length, -1, *after), dim, 0)]
  transfers between devices with their start and end apart: 10 -> 0, of which waited for: 10 -> 0; matrix products, arithmetic and copies ran while one was open for 6% -> 0% of each run, Pallas kernels for 0% -> 0%
where the time goes in v1:
time: 121 us
  Pallas kernels  115 us (95%)
  local copies, waits for them, and re-layouts  4.77 us (4%)
    pallas_call x1, Pallas kernels, per_device(): pl.pallas_call(kernel, out_shape=(jax.ShapeDtypeStruct(flat, F32), jax.Sh...  115 us
    unnamed x2, local copies, waits for them, and re-layouts  3.58 us

profile of v1, /device:TPU:0, one launch (start us, length us, event | category | flops | bytes accessed | tf_op | source)
XLA Modules:
  0.0 120.6 jit_solution(11952439794428328602)
XLA Ops:
  0.6 115.2 %shard_map.112 = (f32[2048,128]{1,0:T(8,128)}, f32[32,1,128]{2,1,0:T(1,128)}, f32[8,128]{1,0:T(8,128)}) custom-call(bf16[80,128,1024]{2,1,0:T(8,128)(2,1)} %tiles_hbm.1, s32[1,80]{1,0:T(1,128)} %bitcast.18, s32[1,32]{1,0:T(1,128)} %bitcast.19, s32[1,32]{1,0:T(1,128)} %bitcast.20, bf16[32,128]{1,0:T(8,128)(2,1)} %bitcast.16, bf16[32,128]{1,0:T(8,128)(2,1)} %bitcast.17, ...), custom_call_target="tpu_custom_call" | custom-call | tf_op jit(solution)/shard_map/pallas_call | solution.py:441
  115.8 1.2 slice.3
  117.0 2.3 %copy.14 = f32[262144]{0:T(1024)} copy(f32[262144]{0:T(1024)} %bitcast.14) | data formatting | bytes 2097152
  119.3 1.3 %copy.15 = f32[4096]{0:T(1024)} copy(f32[4096]{0:T(1024)} %bitcast.15) | data formatting | bytes 32768

commit v2 on v1

--- a/solution.py
+++ b/solution.py
@@ -88,8 +88,6 @@
     rcv_sem,
     zsnd_sem,
     zrcv_sem,
-    gzs_sem,
-    gzr_sem,
     gs_sem,
     gr_sem,
     vs_sem,
@@ -133,7 +131,7 @@
         )
 
     def to_plane(src, dst, ssem, rsem):
-        def go(k, _):
+        for k in range(1, PLANE):
             peer = lax.rem(me + k, PLANE)
             pltpu.make_async_remote_copy(
                 src_ref=src(peer),
@@ -143,9 +141,6 @@
                 device_id=(z, peer),
                 device_id_type=MESH,
             ).start()
-            return 0
-
-        lax.fori_loop(1, PLANE, go, 0)
 
     def to_z(src, dst, ssem, rsem, peer_z):
         pltpu.make_async_remote_copy(
@@ -189,7 +184,7 @@
                 carry = body(p, c, at, carry)
             return carry
 
-        return lax.fori_loop(0, 16, row, start)
+        return lax.fori_loop(0, 16, row, start, unroll=2)
 
     def table(j, p, c, value):
         xtab[j, pl.ds(pl.multiple_of(16 * p, 16), 16), pl.ds(TR * c, TR)] = value.astype(BF16)
@@ -218,6 +213,8 @@
         total = total.astype(BF16)
         for c in range(2):
             snd[it, j, pl.ds(16 * c, 16)] = total[:, TR * c : TR * (c + 1)].reshape(16, 16, TR)
+
+    def columns_out(it, j):
         to_plane(lambda i: snd.at[it, j, i], rcv.at[it, j, me], snd_sem.at[it, j], rcv_sem.at[it, j])
 
     def rows(j):
@@ -225,14 +222,16 @@
         lane = iota((TR, TR), 1)
 
         def group(g, merged):
-            at = pl.ds(pl.multiple_of(GROUP * g, GROUP), GROUP)
-            block = tiles[j, at].reshape(GROUP * TR, LANES)
+            block = tiles[j, pl.ds(GROUP * g, GROUP)].reshape(GROUP * TR, LANES)
             out = dot(block, vsel[...], ((1,), (1,)))
             for k in range(GROUP):
                 merged = jnp.where(lane == GROUP * g + k, out[TR * k : TR * (k + 1)], merged)
             return merged
 
-        macc[...] += lax.fori_loop(0, NG, group, jnp.zeros((TR, TR), F32))
+        merged = jnp.zeros((TR, TR), F32)
+        for g in range(NG):
+            merged = group(g, merged)
+        macc[...] += merged
 
     def rows_done():
         out = dot(omat[...], macc[...], ((1,), (1,)), exact=True)
@@ -246,44 +245,32 @@
         for i in range(1, PLANE):
             total += rcv[it, j, i].astype(F32)
 
-        @pl.when(z == j)
-        def _():
-            zrcv[it, j] = total
-
-        @pl.when(z != j)
-        def _():
-            zsnd[it, j] = total
-            to_z(zsnd.at[it, j], zrcv.at[it, z], zsnd_sem.at[it, j], zrcv_sem.at[it], j)
-
-    def root_sum(it, j):
-        @pl.when(z == j)
-        def _():
-            await_bytes(zrcv.at[it, pl.ds(0, ZN - 1)], zrcv_sem.at[it])
-            total = zrcv[it, 0] + zrcv[it, 1] + zrcv[it, 2] + zrcv[it, 3]
-            grad[it, j, me] = total.astype(BF16)
-            for k in range(1, ZN):
-                to_z(
-                    grad.at[it, j, me],
-                    grad.at[it, j, me],
-                    gzs_sem.at[it],
-                    gzr_sem.at[it, j],
-                    lax.rem(z + k, ZN),
-                )
+        zsnd[it, j] = total
+        zrcv[it, j, z] = total
+        for k in range(1, ZN):
+            to_z(
+                zsnd.at[it, j],
+                zrcv.at[it, j, z],
+                zsnd_sem.at[it, j],
+                zrcv_sem.at[it, j],
+                lax.rem(z + k, ZN),
+            )
 
     def spread(it, j):
-        @pl.when(z != j)
-        def _():
-            await_bytes(grad.at[it, j, me], gzr_sem.at[it, j])
-
+        await_bytes(zrcv.at[it, j, pl.ds(0, ZN - 1)], zrcv_sem.at[it, j])
+        total = zrcv[it, j, 0] + zrcv[it, j, 1] + zrcv[it, j, 2] + zrcv[it, j, 3]
+        grad[it, j, me] = total.astype(BF16)
         to_plane(
             lambda i: grad.at[it, j, me], grad.at[it, j, me], gs_sem.at[it, j], gr_sem.at[it, j]
         )
 
-    def violation_out(it, violated):
+    def violation_in(it, violated):
         part = violated[0:8] + violated[8:16] + violated[16:24] + violated[24:32]
         part = jnp.sum(part, axis=0, keepdims=True)
         vsnd[it] = part
         vrcv[it, me] = part
+
+    def violation_out(it):
         to_plane(lambda i: vsnd.at[it], vrcv.at[it, me], vs_sem.at[it], vr_sem.at[it])
 
     def violation_plane(it):
@@ -333,10 +320,20 @@
             @pl.when(it == 0)
             def _():
                 tile_copy(j).wait()
-                if j == 0:
+
+            columns(it, j)
+            if j == 0:
+
+                @pl.when(it == 0)
+                def _():
                     pl.semaphore_wait(barrier, PLANE - 1 + ZN - 1)
 
-            columns(it, j)
+            columns_out(it, j)
+            if j == 0:
+
+                @pl.when(it > 0)
+                def _():
+                    violation_out(it - 1)
 
         def early_rows(j):
             @pl.when(it == 0)
@@ -345,24 +342,19 @@
 
         plane_sum(it, 0)
         plane_sum(it, 1)
-        root_sum(it, 0)
-        plane_sum(it, 2)
-        root_sum(it, 1)
-        plane_sum(it, 3)
         early_rows(0)
         spread(it, 0)
-        root_sum(it, 2)
+        plane_sum(it, 2)
+        early_rows(1)
         spread(it, 1)
-        root_sum(it, 3)
-        early_rows(1)
+        plane_sum(it, 3)
+        early_rows(2)
 
         @pl.when(it > 0)
         def _():
             violation_plane(it - 1)
 
         spread(it, 2)
-        spread(it, 3)
-        early_rows(2)
         early_rows(3)
 
         @pl.when(it == 0)
@@ -380,9 +372,10 @@
         sigma = STEP * weight
         moved = jnp.zeros((16, TR), F32)
         for j in range(CH):
-            grad_at = grad.at[it, j, pl.ds(0, PLANE - 1)]
-            await_bytes(grad_at, gr_sem.at[it, j])
+            await_bytes(grad.at[it, j, pl.ds(0, PLANE - 1)], gr_sem.at[it, j])
             moved = update(it, j, tau, moved)
+            if j == 0:
+                spread(it, CH - 1)
             rows(j)
 
         @pl.when(it == ITERS - 1)
@@ -393,7 +386,7 @@
         wgt[pl.ds(8, 8), :] = jnp.broadcast_to(change, (8, TR))
         image = rows_done()
         violated = jnp.maximum(bounds[...] - image, 0.0)
-        violation_out(it, violated * violated)
+        violation_in(it, violated * violated)
         dual[pl.ds(0, BLOCKS), :] = jnp.maximum(
             dual[pl.ds(0, BLOCKS), :] + sigma * (bounds[...] - (2.0 * image - img[...])), 0.0
         )
@@ -407,6 +400,7 @@
     for i in range(BLOCKS):
         dsnd[i] = ordered[i : i + 1]
     drcv[me] = dsnd[me]
+    violation_out(ITERS - 1)
     to_plane(lambda i: dsnd.at[i], drcv.at[me], ds_sem, dr_sem)
     violation_plane(ITERS - 1)
     await_bytes(drcv.at[pl.ds(0, PLANE - 1)], dr_sem)
@@ -418,12 +412,8 @@
         for j in range(CH):
             await_bytes(snd.at[it, j, pl.ds(0, PLANE - 1)], snd_sem.at[it, j])
             await_bytes(grad.at[it, j, pl.ds(0, PLANE - 1)], gs_sem.at[it, j])
-
-            @pl.when(z != j)
-            def _():
-                await_bytes(zsnd.at[it, j], zsnd_sem.at[it, j])
-
-        await_bytes(grad.at[it, 0, pl.ds(0, ZN - 1)], gzs_sem.at[it])
+            await_bytes(zrcv.at[it, j, pl.ds(0, ZN - 1)], zsnd_sem.at[it, j])
+
         await_bytes(vrcv.at[it, pl.ds(0, PLANE - 1)], vs_sem.at[it])
         await_bytes(vzrcv.at[it, pl.ds(0, ZN - 1)], vzs_sem.at[it])
         return 0
@@ -431,6 +421,12 @@
     lax.fori_loop(0, ITERS, drain, 0)
     await_bytes(dsnd.at[pl.ds(0, PLANE - 1)], ds_sem)
     pltpu.make_async_copy(x, xo_ref, out_sem).wait()
+
+
+def hand_over(x_ref, dual_ref, weight_ref, x_out, dual_out, weight_out):
+    x_out[...] = x_ref[...]
+    dual_out[...] = dual_ref[...]
+    weight_out[0] = weight_ref[0, 0]
 
 
 def per_device(tiles, col, counts, dest, bounds, dual0, primal, cost, upper):
@@ -467,7 +463,7 @@
             pltpu.VMEM((ITERS, CH, PLANE, 16, TR), BF16),
             pltpu.VMEM((ITERS, CH, PLANE, 16, TR), BF16),
             pltpu.VMEM((ITERS, CH, 16, TR), F32),
-            pltpu.VMEM((ITERS, ZN, 16, TR), F32),
+            pltpu.VMEM((ITERS, CH, ZN, 16, TR), F32),
             pltpu.VMEM((ITERS, CH, PLANE, 16, TR), BF16),
             pltpu.VMEM((ITERS, 1, TR), F32),
             pltpu.VMEM((ITERS, PLANE, 1, TR), F32),
@@ -482,8 +478,6 @@
             dma((ITERS, CH)),
             dma((ITERS, CH)),
             dma((ITERS, CH)),
-            dma((ITERS,)),
-            dma((ITERS,)),
             dma((ITERS, CH)),
             dma((ITERS, CH)),
             dma((ITERS, CH)),
@@ -508,7 +502,16 @@
         cost.reshape(flat),
         upper.reshape(flat),
     )
-    return x_out.reshape(-1), dual_out.reshape(-1), weight[0, :1]
+    return pl.pallas_call(
+        hand_over,
+        out_shape=(
+            jax.ShapeDtypeStruct((NCB * CB,), F32),
+            jax.ShapeDtypeStruct((BLOCKS * TR,), F32),
+            jax.ShapeDtypeStruct((1,), F32),
+        ),
+        in_specs=[vmem, vmem, vmem],
+        out_specs=(vmem, vmem, pl.BlockSpec(memory_space=pltpu.SMEM)),
+    )(x_out.reshape(-1), dual_out.reshape(-1), weight)
 
 
 def solution(mesh):

time: 121 us -> 99.2 us (0.82)
  Pallas kernels: 115 us -> 98.4 us
  local copies, waits for them, and re-layouts: 4.77 us -> 0 us
    pallas_call x1, Pallas kernels: 115 us -> 96.1 us  [per_device(): pl.pallas_call(kernel, out_shape=(jax.ShapeDtypeStruct(flat, F32), jax.Sh...]
    unnamed x2 -> x0, local copies, waits for them, and re-layouts: 3.58 us -> none
    pallas_call x0 -> x1, Pallas kernels: none -> 2.3 us  [per_device(): pl.pallas_call(hand_over, out_shape=(jax.ShapeDtypeStruct((NCB * CB,), F3...]
where the time goes in v2:
time: 99.2 us; the launch traced here: 99 us
  Pallas kernels  98.4 us (99%)
    pallas_call x1, Pallas kernels, per_device(): pl.pallas_call(kernel, out_shape=(jax.ShapeDtypeStruct(flat, F32), jax.Sh...  96.1 us
    pallas_call x1, Pallas kernels, per_device(): pl.pallas_call(hand_over, out_shape=(jax.ShapeDtypeStruct((NCB * CB,), F3...  2.3 us

profile of v2, /device:TPU:0, one launch (start us, length us, event | category | flops | bytes accessed | tf_op | source)
XLA Modules:
  0.0 99.0 jit_solution(8194074595697177775)
XLA Ops:
  0.6 96.1 %shard_map.112 = (f32[2048,128]{1,0:T(8,128)}, f32[32,1,128]{2,1,0:T(1,128)}, f32[8,128]{1,0:T(8,128)}) custom-call(bf16[80,128,1024]{2,1,0:T(8,128)(2,1)} %tiles_hbm.1, s32[1,80]{1,0:T(1,128)} %bitcast.17, s32[1,32]{1,0:T(1,128)} %bitcast.18, s32[1,32]{1,0:T(1,128)} %bitcast.19, bf16[32,128]{1,0:T(8,128)(2,1)} %bitcast.15, bf16[32,128]{1,0:T(8,128)(2,1)} %bitcast.16, ...), custom_call_target="tpu_custom_call" | custom-call | tf_op jit(solution)/shard_map/pallas_call | solution.py:437
  96.7 2.3 %shard_map.113 = (f32[262144]{0:T(1024)}, f32[4096]{0:T(1024)}, f32[1]{0:T(128)}) custom-call(f32[262144]{0:T(1024)} %bitcast.13, f32[4096]{0:T(1024)} %bitcast.14, f32[8,128]{1,0:T(8,128)} %get-tuple-element.8.weight_ref), custom_call_target="tpu_custom_call" | custom-call | tf_op jit(solution)/shard_map/pallas_call | solution.py:505

commit v3 on v2

--- a/solution.py
+++ b/solution.py
@@ -18,6 +18,8 @@
 LANES = CB // CH
 GROUP = 16
 NG = SLOTS // GROUP
+VSLOTS = 32
+CMAT = 64
 PLANE = 32
 ZN = 4
 STEP = 0.3
@@ -66,6 +68,9 @@
     prod,
     macc,
     vsel,
+    vrow,
+    wcol,
+    wide,
     img,
     dual,
     wgt,
@@ -111,28 +116,30 @@
             tiles_hbm.at[:, :, pl.ds(LANES * j, LANES)], tiles.at[j], tile_sem.at[j]
         )
 
-    for j in range(CH):
-        tile_copy(j).start()
-    vec_copies[1].start()
-    vec_copies[2].start()
+    tile_copy(0).start()
+
+    along = [8 * lax.rem(me // 8 + k, 4) for k in range(4)]
+    across = [2 * lax.rem(me // 2 + k, 4) for k in range(4)]
+    cores = [lax.rem(me + k, 2) for k in range(2)]
+    peers = [
+        along[a] + across[b] + cores[c]
+        for hops in (4, 3, 2, 1, 0)
+        for a in range(4)
+        for b in range(4)
+        for c in range(2)
+        if min(a, 4 - a) + min(b, 4 - b) == hops and (a, b, c) != (0, 0, 0)
+    ]
 
     barrier = pltpu.get_barrier_semaphore()
-
-    def greet(k, _):
-        pl.semaphore_signal(
-            barrier, inc=1, device_id=(z, lax.rem(me + k, PLANE)), device_id_type=MESH
-        )
-        return 0
-
-    lax.fori_loop(1, PLANE, greet, 0)
+    for peer in peers:
+        pl.semaphore_signal(barrier, inc=1, device_id=(z, peer), device_id_type=MESH)
     for k in range(1, ZN):
         pl.semaphore_signal(
             barrier, inc=1, device_id=(lax.rem(z + k, ZN), me), device_id_type=MESH
         )
 
     def to_plane(src, dst, ssem, rsem):
-        for k in range(1, PLANE):
-            peer = lax.rem(me + k, PLANE)
+        for peer in peers:
             pltpu.make_async_remote_copy(
                 src_ref=src(peer),
                 dst_ref=dst,
@@ -170,6 +177,7 @@
     omat[...] = owner
     owner = jnp.concatenate([owner, jnp.zeros((TR - BLOCKS, TR), F32)], axis=0)
     otmat[...] = owner.T.astype(BF16)
+    tile_copy(1).start()
     prod[...] = jnp.zeros_like(prod)
     macc[...] = jnp.zeros_like(macc)
     wgt[...] = jnp.ones_like(wgt)
@@ -190,6 +198,10 @@
         xtab[j, pl.ds(pl.multiple_of(16 * p, 16), 16), pl.ds(TR * c, TR)] = value.astype(BF16)
 
     vec_copies[0].wait()
+    tile_copy(2).start()
+    tile_copy(3).start()
+    vec_copies[1].start()
+    vec_copies[2].start()
     for j in range(CH):
 
         def first_table(p, c, at, carry, j=j):
@@ -199,13 +211,30 @@
         pieces(j, first_table, 0)
 
     def columns(it, j):
-        def group(g, _):
-            rows = pl.ds(pl.multiple_of(GROUP * g, GROUP), GROUP)
-            block = tiles[j, rows].reshape(GROUP * TR, LANES)
-            prod[rows, :] = dot(bd[g], block)
-            return 0
-
-        lax.fori_loop(0, NG, group, 0)
+        def by_matmul(g):
+            at = pl.ds(GROUP * g, GROUP)
+            prod[at, :] = dot(bd[g], tiles[j, at].reshape(GROUP * TR, LANES))
+
+        def by_vector(s):
+            if j == 0:
+                spot = wcol[:, s : s + 1]
+                scale = jnp.broadcast_to(spot, (TR, TR))
+                wide[s - CMAT] = scale
+            else:
+                scale = wide[s - CMAT]
+            part = tiles[j, s].astype(F32)
+            for c in range(2):
+                lanes = pl.ds(TR * c, TR)
+                some = part[:, TR * c : TR * (c + 1)] * scale
+                prod[pl.ds(s, 1), lanes] = jnp.sum(some, axis=0, keepdims=True)
+
+        left = list(range(CMAT, SLOTS))
+        groups = CMAT // GROUP
+        share = -(-len(left) // groups)
+        for g in range(groups):
+            by_matmul(g)
+            for s in left[share * g : share * (g + 1)]:
+                by_vector(s)
         full = prod[...]
         high = full.astype(BF16)
         low = (full - high.astype(F32)).astype(BF16)
@@ -218,19 +247,31 @@
         to_plane(lambda i: snd.at[it, j, i], rcv.at[it, j, me], snd_sem.at[it, j], rcv_sem.at[it, j])
 
     def rows(j):
-        vsel[...] = dot(ctmat[...], xtab[j]).astype(BF16)
+        picked = dot(ctmat[...], xtab[j])
+        vsel[...] = picked.astype(BF16)
+        vrow[...] = picked
         lane = iota((TR, TR), 1)
 
-        def group(g, merged):
+        def by_matmul(g, merged):
             block = tiles[j, pl.ds(GROUP * g, GROUP)].reshape(GROUP * TR, LANES)
             out = dot(block, vsel[...], ((1,), (1,)))
             for k in range(GROUP):
                 merged = jnp.where(lane == GROUP * g + k, out[TR * k : TR * (k + 1)], merged)
             return merged
 
+        def by_vector(s, merged):
+            part = tiles[j, s].astype(F32) * vrow[pl.ds(s, 1), :]
+            part = part[:, :TR] + part[:, TR:]
+            return jnp.where(lane == s, jnp.sum(part, axis=1, keepdims=True), merged)
+
         merged = jnp.zeros((TR, TR), F32)
-        for g in range(NG):
-            merged = group(g, merged)
+        left = list(range(SLOTS - VSLOTS, SLOTS))
+        groups = (SLOTS - VSLOTS) // GROUP
+        share = -(-VSLOTS // groups)
+        for g in range(groups):
+            merged = by_matmul(g, merged)
+            for s in left[share * g : share * (g + 1)]:
+                merged = by_vector(s, merged)
         macc[...] += merged
 
     def rows_done():
@@ -311,7 +352,8 @@
     def iteration(it, _):
         chosen = dot(otmat[...], dual[...].astype(BF16))
         line = iota((GROUP, TR), 0)
-        for g in range(NG):
+        wcol[...] = chosen.T
+        for g in range(CMAT // GROUP):
             part = chosen[GROUP * g : GROUP * (g + 1)]
             for k in range(GROUP):
                 bd[g, :, pl.ds(TR * k, TR)] = jnp.where(line == k, part, 0.0).astype(BF16)
@@ -341,6 +383,11 @@
                 rows(j)
 
         plane_sum(it, 0)
+
+        @pl.when(it > 0)
+        def _():
+            violation_plane(it - 1)
+
         plane_sum(it, 1)
         early_rows(0)
         spread(it, 0)
@@ -349,11 +396,6 @@
         spread(it, 1)
         plane_sum(it, 3)
         early_rows(2)
-
-        @pl.when(it > 0)
-        def _():
-            violation_plane(it - 1)
-
         spread(it, 2)
         early_rows(3)
 
@@ -457,6 +499,9 @@
             pltpu.VMEM((TR, LANES), F32),
             pltpu.VMEM((TR, TR), F32),
             pltpu.VMEM((TR, LANES), BF16),
+            pltpu.VMEM((TR, LANES), F32),
+            pltpu.VMEM((TR, TR), F32),
+            pltpu.VMEM((SLOTS - CMAT, TR, TR), F32),
             pltpu.VMEM((BLOCKS, TR), F32),
             pltpu.VMEM((TR, TR), F32),
             pltpu.VMEM((16, TR), F32),

time: 99.2 us -> 87.6 us (0.88)
  Pallas kernels: 98.4 us -> 86.8 us
    pallas_call x1, Pallas kernels: 96.1 us -> 84.5 us  [per_device(): pl.pallas_call(kernel, out_shape=(jax.ShapeDtypeStruct(flat, F32), jax.Sh...]
where the time goes in v3:
time: 87.6 us; the launch traced here: 87.4 us
  Pallas kernels  86.8 us (99%)
    pallas_call x1, Pallas kernels, per_device(): pl.pallas_call(kernel, out_shape=(jax.ShapeDtypeStruct(flat, F32), jax.Sh...  84.5 us
    pallas_call x1, Pallas kernels, per_device(): pl.pallas_call(hand_over, out_shape=(jax.ShapeDtypeStruct((NCB * CB,), F3...  2.3 us

profile of v3, /device:TPU:0, one launch (start us, length us, event | category | flops | bytes accessed | tf_op | source)
XLA Modules:
  0.0 87.4 jit_solution(8573541804010924843)
XLA Ops:
  0.6 84.5 %shard_map.112 = (f32[2048,128]{1,0:T(8,128)}, f32[32,1,128]{2,1,0:T(1,128)}, f32[8,128]{1,0:T(8,128)}) custom-call(bf16[80,128,1024]{2,1,0:T(8,128)(2,1)} %tiles_hbm.1, s32[1,80]{1,0:T(1,128)} %bitcast.17, s32[1,32]{1,0:T(1,128)} %bitcast.18, s32[1,32]{1,0:T(1,128)} %bitcast.19, bf16[32,128]{1,0:T(8,128)(2,1)} %bitcast.15, bf16[32,128]{1,0:T(8,128)(2,1)} %bitcast.16, ...), custom_call_target="tpu_custom_call" | custom-call | tf_op jit(solution)/shard_map/pallas_call | solution.py:479
  85.2 2.3 %shard_map.113 = (f32[262144]{0:T(1024)}, f32[4096]{0:T(1024)}, f32[1]{0:T(128)}) custom-call(f32[262144]{0:T(1024)} %bitcast.13, f32[4096]{0:T(1024)} %bitcast.14, f32[8,128]{1,0:T(8,128)} %get-tuple-element.8.weight_ref), custom_call_target="tpu_custom_call" | custom-call | tf_op jit(solution)/shard_map/pallas_call | solution.py:550

commit v4 on v3

--- a/solution.py
+++ b/solution.py
@@ -44,17 +44,22 @@
 
 def kernel(
     tiles_hbm,
-    col_ref,
-    cnt_ref,
-    dst_ref,
-    bnd_ref,
-    dual0_ref,
+    col_hbm,
+    cnt_hbm,
+    dst_hbm,
+    bnd_hbm,
+    dual0_hbm,
     x_hbm,
     c_hbm,
     u_hbm,
     xo_ref,
     do_ref,
     wo_ref,
+    col_ref,
+    cnt_ref,
+    dst_ref,
+    bnd_ref,
+    dual0_ref,
     tiles,
     x,
     cost,
@@ -88,6 +93,7 @@
     bounds,
     tile_sem,
     vec_sem,
+    small_sem,
     out_sem,
     snd_sem,
     rcv_sem,
@@ -109,14 +115,24 @@
         pltpu.make_async_copy(h, v, vec_sem.at[n])
         for n, (h, v) in enumerate(((x_hbm, x), (c_hbm, cost), (u_hbm, upper)))
     ]
-    vec_copies[0].start()
 
     def tile_copy(j):
         return pltpu.make_async_copy(
             tiles_hbm.at[:, :, pl.ds(LANES * j, LANES)], tiles.at[j], tile_sem.at[j]
         )
 
+    small = (
+        (col_hbm, col_ref),
+        (cnt_hbm, cnt_ref),
+        (dst_hbm, dst_ref),
+        (bnd_hbm, bnd_ref),
+        (dual0_hbm, dual0_ref),
+    )
+    small = [pltpu.make_async_copy(h, v, small_sem.at[n]) for n, (h, v) in enumerate(small)]
+    for copy in small:
+        copy.start()
     tile_copy(0).start()
+    vec_copies[0].start()
 
     along = [8 * lax.rem(me // 8 + k, 4) for k in range(4)]
     across = [2 * lax.rem(me // 2 + k, 4) for k in range(4)]
@@ -133,7 +149,7 @@
     barrier = pltpu.get_barrier_semaphore()
     for peer in peers:
         pl.semaphore_signal(barrier, inc=1, device_id=(z, peer), device_id_type=MESH)
-    for k in range(1, ZN):
+    for k in (2, 1, 3):
         pl.semaphore_signal(
             barrier, inc=1, device_id=(lax.rem(z + k, ZN), me), device_id_type=MESH
         )
@@ -162,6 +178,8 @@
     def await_bytes(ref, sem):
         pltpu.make_async_copy(ref, ref, sem).wait()
 
+    for copy in small:
+        copy.wait()
     cols = jnp.broadcast_to(col_ref[...], (NCB, SLOTS))
     onehot = (cols == iota((NCB, SLOTS), 0)).astype(F32)
     onehot = jnp.concatenate([onehot, jnp.zeros((NCB, TR - SLOTS), F32)], axis=1)
@@ -177,7 +195,6 @@
     omat[...] = owner
     owner = jnp.concatenate([owner, jnp.zeros((TR - BLOCKS, TR), F32)], axis=0)
     otmat[...] = owner.T.astype(BF16)
-    tile_copy(1).start()
     prod[...] = jnp.zeros_like(prod)
     macc[...] = jnp.zeros_like(macc)
     wgt[...] = jnp.ones_like(wgt)
@@ -192,31 +209,25 @@
                 carry = body(p, c, at, carry)
             return carry
 
-        return lax.fori_loop(0, 16, row, start, unroll=2)
+        return lax.fori_loop(0, 16, row, start, unroll=4)
 
     def table(j, p, c, value):
         xtab[j, pl.ds(pl.multiple_of(16 * p, 16), 16), pl.ds(TR * c, TR)] = value.astype(BF16)
 
-    vec_copies[0].wait()
-    tile_copy(2).start()
-    tile_copy(3).start()
-    vec_copies[1].start()
-    vec_copies[2].start()
-    for j in range(CH):
-
-        def first_table(p, c, at, carry, j=j):
+    def first_table(j):
+        def fill(p, c, at, carry):
             table(j, p, c, x[at, :])
             return carry
 
-        pieces(j, first_table, 0)
-
-    def columns(it, j):
+        pieces(j, fill, 0)
+
+    def columns(it, j, first):
         def by_matmul(g):
             at = pl.ds(GROUP * g, GROUP)
             prod[at, :] = dot(bd[g], tiles[j, at].reshape(GROUP * TR, LANES))
 
         def by_vector(s):
-            if j == 0:
+            if first:
                 spot = wcol[:, s : s + 1]
                 scale = jnp.broadcast_to(spot, (TR, TR))
                 wide[s - CMAT] = scale
@@ -288,7 +299,7 @@
 
         zsnd[it, j] = total
         zrcv[it, j, z] = total
-        for k in range(1, ZN):
+        for k in (2, 1, 3):
             to_z(
                 zsnd.at[it, j],
                 zrcv.at[it, j, z],
@@ -321,7 +332,7 @@
             total += vrcv[it, i]
         vzsnd[it] = total
         vzrcv[it, z] = total
-        for k in range(1, ZN):
+        for k in (2, 1, 3):
             to_z(
                 vzsnd.at[it],
                 vzrcv.at[it, z],
@@ -357,47 +368,79 @@
             part = chosen[GROUP * g : GROUP * (g + 1)]
             for k in range(GROUP):
                 bd[g, :, pl.ds(TR * k, TR)] = jnp.where(line == k, part, 0.0).astype(BF16)
-        for j in range(CH):
-
+        @pl.when(it == 0)
+        def _():
+            tile_copy(1).start()
+            tile_copy(0).wait()
+            for j in range(2, CH):
+                tile_copy(j).start()
+            vec_copies[1].start()
+            vec_copies[2].start()
+
+        columns(it, 0, True)
+
+        @pl.when(it == 0)
+        def _():
+            pl.semaphore_wait(barrier, PLANE - 1 + ZN - 1)
+
+        columns_out(it, 0)
+
+        @pl.when(it == 0)
+        def _():
+            vec_copies[0].wait()
+            first_table(0)
+
+        def later(j, _):
             @pl.when(it == 0)
             def _():
+                first_table(j)
                 tile_copy(j).wait()
 
-            columns(it, j)
-            if j == 0:
-
-                @pl.when(it == 0)
-                def _():
-                    pl.semaphore_wait(barrier, PLANE - 1 + ZN - 1)
-
+            columns(it, j, False)
             columns_out(it, j)
-            if j == 0:
-
-                @pl.when(it > 0)
-                def _():
-                    violation_out(it - 1)
+            return 0
+
+        lax.fori_loop(1, CH, later, 0)
 
         def early_rows(j):
             @pl.when(it == 0)
             def _():
                 rows(j)
 
+        @pl.when(it > 0)
+        def _():
+            violation_out(it - 1)
+
         plane_sum(it, 0)
+        early_rows(0)
+        plane_sum(it, 1)
+
+        @pl.when(it == 0)
+        def _():
+            spread(it, 0)
+            plane_sum(it, 2)
+            rows(1)
 
         @pl.when(it > 0)
         def _():
+            plane_sum(it, 2)
+            spread(it, 0)
+            plane_sum(it, 3)
+
+        spread(it, 1)
+
+        @pl.when(it == 0)
+        def _():
+            plane_sum(it, 3)
+            rows(2)
+
+        @pl.when(it > 0)
+        def _():
             violation_plane(it - 1)
 
-        plane_sum(it, 1)
-        early_rows(0)
-        spread(it, 0)
-        plane_sum(it, 2)
-        early_rows(1)
-        spread(it, 1)
-        plane_sum(it, 3)
-        early_rows(2)
         spread(it, 2)
         early_rows(3)
+        spread(it, 3)
 
         @pl.when(it == 0)
         def _():
@@ -413,12 +456,13 @@
         tau = STEP / weight
         sigma = STEP * weight
         moved = jnp.zeros((16, TR), F32)
-        for j in range(CH):
+        def step(j, moved):
             await_bytes(grad.at[it, j, pl.ds(0, PLANE - 1)], gr_sem.at[it, j])
             moved = update(it, j, tau, moved)
-            if j == 0:
-                spread(it, CH - 1)
             rows(j)
+            return moved
+
+        moved = lax.fori_loop(0, CH, step, moved)
 
         @pl.when(it == ITERS - 1)
         def _():
@@ -465,15 +509,34 @@
     pltpu.make_async_copy(x, xo_ref, out_sem).wait()
 
 
-def hand_over(x_ref, dual_ref, weight_ref, x_out, dual_out, weight_out):
-    x_out[...] = x_ref[...]
-    dual_out[...] = dual_ref[...]
-    weight_out[0] = weight_ref[0, 0]
+def hand_over(x_in, dual_in, weight_in, x_out, dual_out, weight_out, x, dual, weight, one, sem):
+    part = NCB * CB // 4
+    ins, outs = [], []
+    for n in range(4):
+        at = pl.ds(part * n, part)
+        ins.append(pltpu.make_async_copy(x_in.at[at], x.at[at], sem.at[n]))
+        outs.append(pltpu.make_async_copy(x.at[at], x_out.at[at], sem.at[6 + n]))
+    ins.append(pltpu.make_async_copy(dual_in, dual, sem.at[4]))
+    outs.append(pltpu.make_async_copy(dual, dual_out, sem.at[10]))
+    last_in = pltpu.make_async_copy(weight_in, weight, sem.at[5])
+    last_out = pltpu.make_async_copy(one, weight_out, sem.at[11])
+    last_in.start()
+    for copy in ins:
+        copy.start()
+    last_in.wait()
+    one[0] = weight[0, 0]
+    last_out.start()
+    for copy, after in zip(ins, outs):
+        copy.wait()
+        after.start()
+    for copy in outs:
+        copy.wait()
+    last_out.wait()
 
 
 def per_device(tiles, col, counts, dest, bounds, dual0, primal, cost, upper):
+    vmem = pl.BlockSpec(memory_space=pltpu.VMEM)
     anywhere = pl.BlockSpec(memory_space=pl.ANY)
-    vmem = pl.BlockSpec(memory_space=pltpu.VMEM)
     dma = pltpu.SemaphoreType.DMA
     flat = (NCB * CB // TR, TR)
     x_out, dual_out, weight = pl.pallas_call(
@@ -483,9 +546,14 @@
             jax.ShapeDtypeStruct((BLOCKS, 1, TR), F32),
             jax.ShapeDtypeStruct((8, TR), F32),
         ),
-        in_specs=[anywhere, vmem, vmem, vmem, vmem, vmem, anywhere, anywhere, anywhere],
+        in_specs=[anywhere] * 9,
         out_specs=(anywhere, vmem, vmem),
         scratch_shapes=[
+            pltpu.VMEM((1, SLOTS), jnp.int32),
+            pltpu.VMEM((1, BLOCKS), jnp.int32),
+            pltpu.VMEM((1, BLOCKS), jnp.int32),
+            pltpu.VMEM((BLOCKS, TR), BF16),
+            pltpu.VMEM((BLOCKS, TR), BF16),
             pltpu.VMEM((CH, SLOTS, TR, LANES), BF16),
             pltpu.VMEM(flat, F32),
             pltpu.VMEM(flat, F32),
@@ -519,6 +587,7 @@
             pltpu.VMEM((BLOCKS, TR), F32),
             dma((CH,)),
             dma((3,)),
+            dma((5,)),
             dma,
             dma((ITERS, CH)),
             dma((ITERS, CH)),
@@ -554,8 +623,15 @@
             jax.ShapeDtypeStruct((BLOCKS * TR,), F32),
             jax.ShapeDtypeStruct((1,), F32),
         ),
-        in_specs=[vmem, vmem, vmem],
-        out_specs=(vmem, vmem, pl.BlockSpec(memory_space=pltpu.SMEM)),
+        in_specs=[anywhere] * 3,
+        out_specs=(anywhere, anywhere, anywhere),
+        scratch_shapes=[
+            pltpu.VMEM((NCB * CB,), F32),
+            pltpu.VMEM((BLOCKS * TR,), F32),
+            pltpu.VMEM((8, TR), F32),
+            pltpu.SMEM((1,), F32),
+            dma((12,)),
+        ],
     )(x_out.reshape(-1), dual_out.reshape(-1), weight)
 
 

time: 87.6 us -> 82.8 us (0.945)
  Pallas kernels: 86.8 us -> 82 us
    pallas_call x1, Pallas kernels: 84.5 us -> 80 us  [per_device(): pl.pallas_call(kernel, out_shape=(jax.ShapeDtypeStruct(flat, F32), jax.Sh...]
where the time goes in v4:
time: 82.8 us; the launch traced here: 82.6 us
  Pallas kernels  82 us (99%)
    pallas_call x1, Pallas kernels, per_device(): pl.pallas_call(kernel, out_shape=(jax.ShapeDtypeStruct(flat, F32), jax.Sh...  80 us
    pallas_call x1, Pallas kernels, per_device(): pl.pallas_call(hand_over, out_shape=(jax.ShapeDtypeStruct((NCB * CB,), F3...  2.03 us

profile of v4, /device:TPU:0, one launch (start us, length us, event | category | flops | bytes accessed | tf_op | source)
XLA Modules:
  0.0 82.6 jit_solution(15695718521516762682)
XLA Ops:
  0.6 80.0 %shard_map.112 = (f32[2048,128]{1,0:T(8,128)}, f32[32,1,128]{2,1,0:T(1,128)}, f32[8,128]{1,0:T(8,128)}) custom-call(bf16[80,128,1024]{2,1,0:T(8,128)(2,1)} %tiles_hbm.1, s32[1,80]{1,0:T(1,128)} %bitcast.17, s32[1,32]{1,0:T(1,128)} %bitcast.18, s32[1,32]{1,0:T(1,128)} %bitcast.19, bf16[32,128]{1,0:T(8,128)(2,1)} %bitcast.15, bf16[32,128]{1,0:T(8,128)(2,1)} %bitcast.16, ...), custom_call_target="tpu_custom_call" | custom-call | tf_op jit(solution)/shard_map/pallas_call | solution.py:542
  80.6 2.0 %shard_map.113 = (f32[262144]{0:T(1024)}, f32[4096]{0:T(1024)}, f32[1]{0:T(128)}) custom-call(f32[262144]{0:T(1024)} %bitcast.13, f32[4096]{0:T(1024)} %bitcast.14, f32[8,128]{1,0:T(8,128)} %get-tuple-element.8.weight_in), custom_call_target="tpu_custom_call" | custom-call | tf_op jit(solution)/shard_map/pallas_call | solution.py:619

commit v5 on v4

--- a/solution.py
+++ b/solution.py
@@ -18,7 +18,8 @@
 LANES = CB // CH
 GROUP = 16
 NG = SLOTS // GROUP
-VSLOTS = 32
+VSLOTS = 40
+RGROUP = 8
 CMAT = 64
 PLANE = 32
 ZN = 4
@@ -95,6 +96,7 @@
     vec_sem,
     small_sem,
     out_sem,
+    last_sem,
     snd_sem,
     rcv_sem,
     zsnd_sem,
@@ -192,7 +194,8 @@
     ends = dot(upto, counts, ((1,), (1,)))
     slot = iota((BLOCKS, TR), 1).astype(F32)
     owner = jnp.where((starts <= slot) & (slot < ends), 1.0, 0.0)
-    omat[...] = owner
+    omat[:, :TR] = owner.astype(BF16)
+    omat[:, TR:] = owner.astype(BF16)
     owner = jnp.concatenate([owner, jnp.zeros((TR - BLOCKS, TR), F32)], axis=0)
     otmat[...] = owner.T.astype(BF16)
     prod[...] = jnp.zeros_like(prod)
@@ -264,10 +267,10 @@
         lane = iota((TR, TR), 1)
 
         def by_matmul(g, merged):
-            block = tiles[j, pl.ds(GROUP * g, GROUP)].reshape(GROUP * TR, LANES)
+            block = tiles[j, pl.ds(RGROUP * g, RGROUP)].reshape(RGROUP * TR, LANES)
             out = dot(block, vsel[...], ((1,), (1,)))
-            for k in range(GROUP):
-                merged = jnp.where(lane == GROUP * g + k, out[TR * k : TR * (k + 1)], merged)
+            for k in range(RGROUP):
+                merged = jnp.where(lane == RGROUP * g + k, out[TR * k : TR * (k + 1)], merged)
             return merged
 
         def by_vector(s, merged):
@@ -277,7 +280,7 @@
 
         merged = jnp.zeros((TR, TR), F32)
         left = list(range(SLOTS - VSLOTS, SLOTS))
-        groups = (SLOTS - VSLOTS) // GROUP
+        groups = (SLOTS - VSLOTS) // RGROUP
         share = -(-VSLOTS // groups)
         for g in range(groups):
             merged = by_matmul(g, merged)
@@ -286,7 +289,10 @@
         macc[...] += merged
 
     def rows_done():
-        out = dot(omat[...], macc[...], ((1,), (1,)), exact=True)
+        full = macc[...]
+        high = full.astype(BF16)
+        low = (full - high.astype(F32)).astype(BF16)
+        out = dot(omat[...], jnp.concatenate([high, low], axis=1), ((1,), (1,)))
         macc[...] = jnp.zeros_like(macc)
         return out
 
@@ -481,18 +487,21 @@
 
     lax.fori_loop(0, ITERS, iteration, 0)
 
+    violation_out(ITERS - 1)
+
     hot = jnp.broadcast_to(dst_ref[...], (BLOCKS, BLOCKS)) == iota((BLOCKS, BLOCKS), 0)
     ordered = dot(hot.astype(F32), dual[pl.ds(0, BLOCKS), :], exact=True)
     for i in range(BLOCKS):
         dsnd[i] = ordered[i : i + 1]
     drcv[me] = dsnd[me]
-    violation_out(ITERS - 1)
     to_plane(lambda i: dsnd.at[i], drcv.at[me], ds_sem, dr_sem)
     violation_plane(ITERS - 1)
     await_bytes(drcv.at[pl.ds(0, PLANE - 1)], dr_sem)
-    do_ref[...] = drcv[...]
+    dual_out = pltpu.make_async_copy(drcv, do_ref, last_sem.at[0])
+    dual_out.start()
     new_weight(ITERS - 1)
-    wo_ref[...] = wgt[pl.ds(0, 8), :]
+    weight_out = pltpu.make_async_copy(wgt.at[pl.ds(0, 8), :], wo_ref, last_sem.at[1])
+    weight_out.start()
 
     def drain(it, _):
         for j in range(CH):
@@ -507,6 +516,8 @@
     lax.fori_loop(0, ITERS, drain, 0)
     await_bytes(dsnd.at[pl.ds(0, PLANE - 1)], ds_sem)
     pltpu.make_async_copy(x, xo_ref, out_sem).wait()
+    dual_out.wait()
+    weight_out.wait()
 
 
 def hand_over(x_in, dual_in, weight_in, x_out, dual_out, weight_out, x, dual, weight, one, sem):
@@ -535,7 +546,6 @@
 
 
 def per_device(tiles, col, counts, dest, bounds, dual0, primal, cost, upper):
-    vmem = pl.BlockSpec(memory_space=pltpu.VMEM)
     anywhere = pl.BlockSpec(memory_space=pl.ANY)
     dma = pltpu.SemaphoreType.DMA
     flat = (NCB * CB // TR, TR)
@@ -547,7 +557,7 @@
             jax.ShapeDtypeStruct((8, TR), F32),
         ),
         in_specs=[anywhere] * 9,
-        out_specs=(anywhere, vmem, vmem),
+        out_specs=(anywhere, anywhere, anywhere),
         scratch_shapes=[
             pltpu.VMEM((1, SLOTS), jnp.int32),
             pltpu.VMEM((1, BLOCKS), jnp.int32),
@@ -561,7 +571,7 @@
             pltpu.VMEM((CH, NCB, LANES), BF16),
             pltpu.VMEM((NCB, TR), BF16),
             pltpu.VMEM((TR, NCB), BF16),
-            pltpu.VMEM((BLOCKS, TR), F32),
+            pltpu.VMEM((BLOCKS, 2 * TR), BF16),
             pltpu.VMEM((TR, TR), BF16),
             pltpu.VMEM((NG, GROUP, GROUP * TR), BF16),
             pltpu.VMEM((TR, LANES), F32),
@@ -589,6 +599,7 @@
             dma((3,)),
             dma((5,)),
             dma,
+            dma((2,)),
             dma((ITERS, CH)),
             dma((ITERS, CH)),
             dma((ITERS, CH)),

time: 82.8 us -> 81.4 us (0.983)
  Pallas kernels: 82 us -> 80.6 us
    pallas_call x1, Pallas kernels: 80 us -> 78.6 us  [per_device(): pl.pallas_call(kernel, out_shape=(jax.ShapeDtypeStruct(flat, F32), jax.Sh...]
where the time goes in v5:
time: 81.4 us; the launch traced here: 81.2 us
  Pallas kernels  80.6 us (99%)
    pallas_call x1, Pallas kernels, per_device(): pl.pallas_call(kernel, out_shape=(jax.ShapeDtypeStruct(flat, F32), jax.Sh...  78.6 us
    pallas_call x1, Pallas kernels, per_device(): pl.pallas_call(hand_over, out_shape=(jax.ShapeDtypeStruct((NCB * CB,), F3...  2.03 us

profile of v5, /device:TPU:0, one launch (start us, length us, event | category | flops | bytes accessed | tf_op | source)
XLA Modules:
  0.0 81.2 jit_solution(15270480002602436064)
XLA Ops:
  0.6 78.6 %shard_map.112 = (f32[2048,128]{1,0:T(8,128)}, f32[32,1,128]{2,1,0:T(1,128)}, f32[8,128]{1,0:T(8,128)}) custom-call(bf16[80,128,1024]{2,1,0:T(8,128)(2,1)} %tiles_hbm.1, s32[1,80]{1,0:T(1,128)} %bitcast.17, s32[1,32]{1,0:T(1,128)} %bitcast.18, s32[1,32]{1,0:T(1,128)} %bitcast.19, bf16[32,128]{1,0:T(8,128)(2,1)} %bitcast.15, bf16[32,128]{1,0:T(8,128)(2,1)} %bitcast.16, ...), custom_call_target="tpu_custom_call" | custom-call | tf_op jit(solution)/shard_map/pallas_call | solution.py:552
  79.2 2.0 %shard_map.113 = (f32[262144]{0:T(1024)}, f32[4096]{0:T(1024)}, f32[1]{0:T(128)}) custom-call(f32[262144]{0:T(1024)} %bitcast.13, f32[4096]{0:T(1024)} %bitcast.14, f32[8,128]{1,0:T(8,128)} %get-tuple-element.8.weight_in), custom_call_target="tpu_custom_call" | custom-call | tf_op jit(solution)/shard_map/pallas_call | solution.py:630

commit v6 on v5

--- a/solution.py
+++ b/solution.py
@@ -212,7 +212,7 @@
                 carry = body(p, c, at, carry)
             return carry
 
-        return lax.fori_loop(0, 16, row, start, unroll=4)
+        return lax.fori_loop(0, 16, row, start, unroll=8)
 
     def table(j, p, c, value):
         xtab[j, pl.ds(pl.multiple_of(16 * p, 16), 16), pl.ds(TR * c, TR)] = value.astype(BF16)

time: 81.4 us -> 81.4 us (level)
  no operation moved by 1% of the time
where the time goes in v6:
time: 81.4 us; the launch traced here: 81.3 us
  Pallas kernels  80.6 us (99%)
    pallas_call x1, Pallas kernels, per_device(): pl.pallas_call(kernel, out_shape=(jax.ShapeDtypeStruct(flat, F32), jax.Sh...  78.6 us
    pallas_call x1, Pallas kernels, per_device(): pl.pallas_call(hand_over, out_shape=(jax.ShapeDtypeStruct((NCB * CB,), F3...  2.03 us

profile of v6, /device:TPU:0, one launch (start us, length us, event | category | flops | bytes accessed | tf_op | source)
XLA Modules:
  0.0 81.3 jit_solution(2285354858428718897)
XLA Ops:
  0.6 78.6 %shard_map.112 = (f32[2048,128]{1,0:T(8,128)}, f32[32,1,128]{2,1,0:T(1,128)}, f32[8,128]{1,0:T(8,128)}) custom-call(bf16[80,128,1024]{2,1,0:T(8,128)(2,1)} %tiles_hbm.1, s32[1,80]{1,0:T(1,128)} %bitcast.17, s32[1,32]{1,0:T(1,128)} %bitcast.18, s32[1,32]{1,0:T(1,128)} %bitcast.19, bf16[32,128]{1,0:T(8,128)(2,1)} %bitcast.15, bf16[32,128]{1,0:T(8,128)(2,1)} %bitcast.16, ...), custom_call_target="tpu_custom_call" | custom-call | tf_op jit(solution)/shard_map/pallas_call | solution.py:552
  79.2 2.0 %shard_map.113 = (f32[262144]{0:T(1024)}, f32[4096]{0:T(1024)}, f32[1]{0:T(128)}) custom-call(f32[262144]{0:T(1024)} %bitcast.13, f32[4096]{0:T(1024)} %bitcast.14, f32[8,128]{1,0:T(8,128)} %get-tuple-element.8.weight_in), custom_call_target="tpu_custom_call" | custom-call | tf_op jit(solution)/shard_map/pallas_call | solution.py:630
